TPU v7x, 128 devices: a whole 4x4x4 slice. The times are simulated.
128 devices in a mesh: state: 16 (over y_hi, x, core), dp: 8 (over y_lo, z).
Axes of the slice: x: 4, y: 4 (y_hi: 2, y_lo: 2; y = y_hi * 2 + y_lo), z: 4, core: 2. Of those that a mesh axis runs over, the one named last changes fastest.
Arguments:
- state_ensemble: float32 [32768, 256], P('state'), may hold values from -80 to 80, as said below
- predicted_data: float32 [65536, 256], P(('state', 'dp')), may hold values from -125 to 125, as said below
- innovations: bfloat16 [65536, 256], P(('state', 'dp')), may hold values from -6 to 6
Outputs:
- increment: float32 [32768, 256], P(('state', 'dp'))
Inputs may be any that keep to these rules, and one draw needn't show every extreme that they name: `state_ensemble`: finite values. `predicted_data`: finite values.
All inputs are finite; a program needn't handle non-finite values.
Results may differ from a plain program's by a relative error of at most 0.0042.
Values may be sent and summed in bfloat16 or wider, within the bound.
No kernel may reach another device: no remote copies, remote signals or barrier semaphores. Data moves between devices by JAX's collectives and lax.ppermute only.
A program may use at most 64 MiB of HBM per device.

v0:
```python
import jax
import jax.numpy as jnp
from jax import lax
from jax.experimental import pallas as pl
from jax.experimental.pallas import tpu as pltpu
from jax.sharding import PartitionSpec as P


AXES = ("state", "dp")
VMEM = pl.BlockSpec(memory_space=pltpu.VMEM)
HBM = pl.BlockSpec(memory_space=pltpu.HBM)
LIMIT = 24 << 20


def place(i):
    s, d = divmod(i, 8)
    y_hi, rest = divmod(s, 8)
    x, core = divmod(rest, 2)
    y_lo, z = divmod(d, 4)
    return x, y_hi * 2 + y_lo, z, core


def index(x, y, z, core):
    x, y, z = x % 4, y % 4, z % 4
    return ((y // 2) * 8 + x * 2 + core) * 8 + (y % 2) * 4 + z


def sent(value, to):
    return lax.ppermute(value, AXES, [(i, index(*to(*place(i)))) for i in range(128)])


def x_turn(x, y, z, core):
    return x + 1 - 2 * core, y, z, core


def x_back(x, y, z, core):
    return x - 1 + 2 * core, y, z, core


def y_across(x, y, z, core):
    return x, 3 - y, z, core


def other_core(x, y, z, core):
    return x, y, z, 1 - core


def standard(values):
    members = values.shape[1]
    anomalies = values - jnp.mean(values, axis=1, keepdims=True)
    spread = jnp.sqrt(jnp.sum(anomalies * anomalies, axis=1, keepdims=True) / (members - 1) + 1e-06)
    return (anomalies / spread).astype(jnp.bfloat16), spread


def cost(flops, size):
    return pl.CostEstimate(flops=flops, bytes_accessed=size, transcendentals=0)


def pack_data(predicted, innovations):
    rows, members = predicted.shape

    def body(p_hbm, i_hbm, o_ref, p_ref, sems):
        values = pltpu.make_async_copy(p_hbm, p_ref, sems.at[0])
        copied = pltpu.make_async_copy(i_hbm, o_ref.at[:, members:], sems.at[1])
        values.start()
        copied.start()
        values.wait()
        o_ref[:, 0:members] = standard(p_ref[...])[0]
        copied.wait()

    return pl.pallas_call(
        body,
        out_shape=jax.ShapeDtypeStruct((rows, 2 * members), jnp.bfloat16),
        in_specs=[HBM] * 2,
        out_specs=VMEM,
        scratch_shapes=[pltpu.VMEM((rows, members), jnp.float32), pltpu.SemaphoreType.DMA((2,))],
        compiler_params=pltpu.CompilerParams(vmem_limit_bytes=LIMIT),
        cost_estimate=cost(1 << 20, 1 << 20),
        name="pack_data",
    )(predicted, innovations)


def prepare_state(state, own):
    rows, members = state.shape
    count = rows // own

    def body(s_hbm, o_ref, w_ref, s_ref, sems):
        mine = lax.axis_index("dp")
        copies = []
        for i in range(count):
            part = slice(i * own, (i + 1) * own)
            copies.append(pltpu.make_async_copy(s_hbm.at[part, :], s_ref.at[part, :], sems.at[i]))
            copies[i].start()
        for i in range(count):
            part = slice(i * own, (i + 1) * own)
            copies[i].wait()
            std, spread = standard(s_ref[part, :])
            o_ref[part, :] = std

            @pl.when(i == mine)
            def _():
                w_ref[...] = jnp.broadcast_to(spread, (own, members))

    return pl.pallas_call(
        body,
        out_shape=(
            jax.ShapeDtypeStruct((rows, members), jnp.bfloat16),
            jax.ShapeDtypeStruct((own, members), jnp.float32),
        ),
        in_specs=[HBM],
        out_specs=(VMEM, VMEM),
        scratch_shapes=[pltpu.VMEM((rows, members), jnp.float32), pltpu.SemaphoreType.DMA((count,))],
        compiler_params=pltpu.CompilerParams(vmem_limit_bytes=LIMIT),
        cost_estimate=cost(1 << 24, 1 << 22),
        name="prepare_state",
    )(state)


def tile_sum(state, chunks, start, members, width=256):
    total = start
    for chunk in chunks:
        for c in range(0, chunk.shape[0], width):
            correl = lax.dot_general(
                state,
                chunk[c : c + width, 0:members],
                (((1,), (1,)), ((), ())),
                preferred_element_type=jnp.float32,
            ) * (1.0 / (members - 1))
            localized = (correl * correl * correl).astype(jnp.bfloat16)
            part = jnp.dot(localized, chunk[c : c + width, members:], preferred_element_type=jnp.float32)
            total = part if total is None else total + part
    return total


def half_start(far, half):
    lo = lax.axis_index("dp") // 4
    return (1 - lo if far else lo) * half


def add_chunks(parts, chunks, sent_kinds=(), tile=1024):
    members = chunks[0].shape[1] // 2
    half = parts[0][1].shape[0] // 2
    kinds = [jnp.bfloat16 if k in sent_kinds else jnp.float32 for k in range(len(parts))]
    operands, aliases, places = [], {}, []
    for k, (start, state, far) in enumerate(parts):
        if start is not None and kinds[k] == jnp.float32:
            aliases[len(operands)] = k
        if start is not None:
            operands.append(start)
        states = [i for i, o in enumerate(operands) if o is state]
        places.append((None if start is None else len(operands) - 1, len(operands) if not states else states[0], far))
        if not states:
            operands.append(state)
    count = len(operands)
    operands += chunks

    def body(*refs):
        x_refs, o_refs = refs[count : len(operands)], refs[len(operands) :]
        for (start_at, state_at, far), o_ref in zip(places, o_refs):
            base = half_start(far, half)

            def step(i, _):
                there = pl.ds(pl.multiple_of(i * tile, tile), tile)
                part = pl.ds(pl.multiple_of(base + i * tile, tile), tile)
                start = None if start_at is None else refs[start_at][there, :]
                total = tile_sum(refs[state_at][part, :], x_refs, start, members)
                o_ref[there, :] = total.astype(o_ref.dtype)
                return 0

            if tile == half:
                step(0, 0)
            else:
                lax.fori_loop(0, half // tile, step, 0)

    return pl.pallas_call(
        body,
        out_shape=[jax.ShapeDtypeStruct((half, members), kind) for kind in kinds],
        in_specs=[VMEM] * len(operands),
        out_specs=[VMEM] * len(parts),
        input_output_aliases=aliases,
        compiler_params=pltpu.CompilerParams(vmem_limit_bytes=LIMIT),
        cost_estimate=cost(4 * len(parts) * half * members * 512 * len(chunks), 1 << 22),
    )(*operands)


def last_chunks(running, handed, state, chunks, own, far, steps):
    members = running.shape[1]
    count = len(chunks)

    def body(start_ref, handed_ref, s_ref, *refs):
        x_refs, o_refs = refs[:count], refs[count:]
        z = lax.rem(lax.axis_index("dp"), 4)
        base = half_start(far, running.shape[0])
        rows = [pl.multiple_of(lax.rem(z + k, 4) * own, own) for k in steps]
        totals = [start_ref[pl.ds(r, own), :] + handed_ref[pl.ds(r, own), :].astype(jnp.float32) for r in rows]
        if count:
            state_rows = jnp.concatenate([s_ref[pl.ds(base + r, own), :] for r in rows], axis=0)
            total = tile_sum(state_rows, x_refs, jnp.concatenate(totals, axis=0), members)
            totals = [total[j * own : (j + 1) * own, :] for j in range(len(steps))]
        for total, o_ref in zip(totals, o_refs):
            o_ref[...] = total.astype(o_ref.dtype)

    operands = [running, handed, state, *chunks]
    return pl.pallas_call(
        body,
        out_shape=[
            jax.ShapeDtypeStruct((own, members), jnp.bfloat16 if far or k else jnp.float32) for k in steps
        ],
        in_specs=[VMEM] * len(operands),
        out_specs=[VMEM] * len(steps),
        compiler_params=pltpu.CompilerParams(vmem_limit_bytes=LIMIT),
        cost_estimate=cost(4 * len(steps) * own * members * 512 * count + (1 << 20), 1 << 22),
    )(*operands)


def finish(spread, own_block, blocks):
    def body(w_ref, f_ref, *refs):
        total = f_ref[...]
        for ref in refs[:-1]:
            total = total + ref[...].astype(jnp.float32)
        refs[-1][...] = w_ref[...] * total

    return pl.pallas_call(
        body,
        out_shape=jax.ShapeDtypeStruct(own_block.shape, jnp.float32),
        in_specs=[VMEM] * (2 + len(blocks)),
        out_specs=VMEM,
        compiler_params=pltpu.CompilerParams(vmem_limit_bytes=LIMIT),
        cost_estimate=cost(1 << 20, 1 << 20),
        name="finish",
    )(spread, own_block, *blocks)


def update(state_ensemble, predicted_data, innovations):
    own = state_ensemble.shape[0] // 8
    x0 = pack_data(predicted_data, innovations)
    p1a = sent(x0, x_turn)
    y0 = sent(x0, y_across)
    s, spread = prepare_state(state_ensemble, own)
    t = sent(s, other_core)
    p1b = sent(x0, x_back)
    p2 = sent(p1a, x_turn)
    q1a = sent(y0, x_turn)
    q1b = sent(y0, x_back)
    y2 = sent(p2, y_across)
    early = [(None, s, True), (None, t, True), (None, s, False), (None, t, False)]
    fs, ft, ns, nt = add_chunks(early, [x0, p1a])
    ns, nt = add_chunks([(ns, s, False), (nt, t, False)], [p1b, y0])
    fs, ft = add_chunks([(fs, s, True), (ft, t, True)], [p1b, y0])
    fs, ft = add_chunks([(fs, s, True), (ft, t, True)], [p2, q1a])
    ns, nt = add_chunks([(ns, s, False), (nt, t, False)], [p2, q1a])
    fs, ft = add_chunks([(fs, s, True), (ft, t, True)], [q1b], sent_kinds=(1,))
    fh = sent(ft, other_core)
    ns, nt = add_chunks([(ns, s, False), (nt, t, False)], [q1b], sent_kinds=(1,))
    nh = sent(nt, other_core)
    y2s = sent(y2, other_core)
    (fs,) = add_chunks([(fs, s, True)], [y2])
    blocks = {}
    blocks[1, 2], blocks[1, 1] = last_chunks(fs, fh, s, [y2s], own, True, (2, 1))
    blocks[1, 3], blocks[1, 0] = last_chunks(fs, fh, s, [y2s], own, True, (3, 0))
    near = last_chunks(ns, nh, s, [y2, y2s], own, False, (1, 3, 2, 0))
    blocks[0, 1], blocks[0, 3], blocks[0, 2], mine = near
    arrived = []
    for (across, k), block in blocks.items():
        arrived.append(sent(block, lambda x, y, z, core: (x, y ^ across, z + k, core)))
    return finish(spread, mine, arrived)


def solution(mesh):
    in_specs = (P("state", None), P(("state", "dp"), None), P(("state", "dp"), None))
    out_specs = P(("state", "dp"), None)
    return jax.shard_map(update, mesh=mesh, in_specs=in_specs, out_specs=out_specs, check_vma=False)
```

profile of v0, /device:TPU:1, one launch (start us, length us, event | category | flops | bytes accessed | tf_op | source)
XLA Modules:
  0.0 81.2 jit_solution(16633565973051235113)
XLA Ops:
  0.0 1.6 %copy-done = f32[2048,256]{1,0:T(8,128)S(1)} copy-done((f32[2048,256]{1,0:T(8,128)S(1)}, f32[2048,256]{1,0:T(8,128)}, u32[]{:S(2)}) %copy-start) | copy-done | bytes 2097176
  1.6 2.0 %prepare_state.1 = (bf16[2048,256]{1,0:T(8,128)(2,1)S(1)}, f32[256,256]{1,0:T(8,128)S(1)}) custom-call(f32[2048,256]{1,0:T(8,128)S(1)} %copy-done), custom_call_target="tpu_custom_call" | custom-call | flops 16777216 | bytes 4194304 | tf_op jit(solution)/shard_map/prepare_state/pallas_call | solution.py:104
  3.6 1.5 %collective-permute-start = (bf16[2048,256]{1,0:T(8,128)(2,1)S(1)}, bf16[2048,256]{1,0:T(8,128)(2,1)S(1)}, u32[]{:S(2)}, u32[]{:S(2)}) collective-permute-start(bf16[2048,256]{1,0:T(8,128)(2,1)S(1)} %get-tuple-element.32.refs_0_.refs_1_.s_ref), channel_id=1, source_target_pairs={{0,8},{1,9},{2,10},{3,11},{4,12},{5,13},{6,14},{7,15},{8,0},{9,1},... | collective-permute-start | bytes 3145736 | tf_op jit(solution)/shard_map/ppermute | solution.py:29
  5.4 2.7 %collective-permute-start.1 = (bf16[512,512]{1,0:T(8,128)(2,1)S(1)}, bf16[512,512]{1,0:T(8,128)(2,1)S(1)}, u32[]{:S(2)}, u32[]{:S(2)}) collective-permute-start(bf16[512,512]{1,0:T(8,128)(2,1)S(1)} %pack_data.1.refs_2_), channel_id=1, source_target_pairs={{0,16},{1,17},{2,18},{3,19},{4,20},{5,21},{6,22},{7,23},{8,56},{9,... | collective-permute-start | bytes 1572872 | tf_op jit(solution)/shard_map/ppermute | solution.py:29
  8.1 2.7 %collective-permute-start.3 = (bf16[512,512]{1,0:T(8,128)(2,1)S(1)}, bf16[512,512]{1,0:T(8,128)(2,1)S(1)}, u32[]{:S(2)}, u32[]{:S(2)}) collective-permute-start(bf16[512,512]{1,0:T(8,128)(2,1)S(1)} %pack_data.1.refs_2_), channel_id=1, source_target_pairs={{0,68},{1,69},{2,70},{3,71},{4,64},{5,65},{6,66},{7,67},{8,76},{9,... | collective-permute-start | bytes 1572872 | tf_op jit(solution)/shard_map/ppermute | solution.py:29
  10.8 3.4 %collective-permute-done.1.refs_3_ = bf16[512,512]{1,0:T(8,128)(2,1)S(1)} collective-permute-done((bf16[512,512]{1,0:T(8,128)(2,1)S(1)}, bf16[512,512]{1,0:T(8,128)(2,1)S(1)}, u32[]{:S(2)}, u32[]{:S(2)}) %collective-permute-start.1) | collective-permute-done | bytes 524320 | tf_op jit(solution)/shard_map/ppermute | solution.py:29
  14.2 3.4 %collective-permute-start.4 = (bf16[512,512]{1,0:T(8,128)(2,1)S(1)}, bf16[512,512]{1,0:T(8,128)(2,1)S(1)}, u32[]{:S(2)}, u32[]{:S(2)}) collective-permute-start(bf16[512,512]{1,0:T(8,128)(2,1)S(1)} %collective-permute-done.1.refs_3_), channel_id=1, source_target_pairs={{0,16},{1,17},{2,18},{3,19},{4,20},{5,21},{6,22},{7,23},{8,56},{9,... | collective-permute-start | bytes 1572872 | tf_op jit(solution)/shard_map/ppermute | solution.py:29
  17.6 5.1 %collective-permute-done.3.refs_5_ = bf16[512,512]{1,0:T(8,128)(2,1)S(1)} collective-permute-done((bf16[512,512]{1,0:T(8,128)(2,1)S(1)}, bf16[512,512]{1,0:T(8,128)(2,1)S(1)}, u32[]{:S(2)}, u32[]{:S(2)}) %collective-permute-start.3) | collective-permute-done | bytes 524320 | tf_op jit(solution)/shard_map/ppermute | solution.py:29
  24.2 4.9 %shard_map.37 = (f32[1024,256]{1,0:T(8,128)S(1)}, f32[1024,256]{1,0:T(8,128)S(1)}, f32[1024,256]{1,0:T(8,128)S(1)}, f32[1024,256]{1,0:T(8,128)S(1)}) custom-call(bf16[2048,256]{1,0:T(8,128)(2,1)S(1)} %get-tuple-element.32.refs_0_.refs_1_.s_ref, bf16[2048,256]{1,0:T(8,128)(2,1)S(1)} %collective-permute-done.refs_1_.refs_3_, ...), custom_call_target="tpu_custom_call" | custom-call | flops 4294967296 | bytes 4194304 | tf_op jit(solution)/shard_map/pallas_call | solution.py:175
  29.2 3.0 %collective-permute-start.8 = (bf16[512,512]{1,0:T(8,128)(2,1)S(1)}, bf16[512,512]{1,0:T(8,128)(2,1)S(1)}, u32[]{:S(2)}, u32[]{:S(2)}) collective-permute-start(bf16[512,512]{1,0:T(8,128)(2,1)S(1)} %collective-permute-done.4.refs_4_), channel_id=1, source_target_pairs={{0,68},{1,69},{2,70},{3,71},{4,64},{5,65},{6,66},{7,67},{8,76},{9,... | collective-permute-start | bytes 1572872 | tf_op jit(solution)/shard_map/ppermute | solution.py:29
  32.8 2.9 %shard_map.42 = (f32[1024,256]{1,0:T(8,128)S(1)}, f32[1024,256]{1,0:T(8,128)S(1)}) custom-call(f32[1024,256]{1,0:T(8,128)S(1)} %get-tuple-element.42.refs_0_, bf16[2048,256]{1,0:T(8,128)(2,1)S(1)} %get-tuple-element.32.refs_0_.refs_1_.s_ref, f32[1024,256]{1,0:T(8,128)S(1)} %get-tuple-element.43.refs_2_, ...), custom_call_target="tpu_custom_call", output_to_operand_aliasing={{0}: (0, {}), {1}: (2, {})} | custom-call | flops 2147483648 | bytes 4194304 | tf_op jit(solution)/shard_map/pallas_call | solution.py:175
  35.7 3.2 %collective-permute-done.5.refs_5_ = bf16[512,512]{1,0:T(8,128)(2,1)S(1)} collective-permute-done((bf16[512,512]{1,0:T(8,128)(2,1)S(1)}, bf16[512,512]{1,0:T(8,128)(2,1)S(1)}, u32[]{:S(2)}, u32[]{:S(2)}) %collective-permute-start.5) | collective-permute-done | bytes 524320 | tf_op jit(solution)/shard_map/ppermute | solution.py:29
  38.9 2.9 %shard_map.43 = (f32[1024,256]{1,0:T(8,128)S(1)}, f32[1024,256]{1,0:T(8,128)S(1)}) custom-call(f32[1024,256]{1,0:T(8,128)S(1)} %get-tuple-element.44.refs_0_, bf16[2048,256]{1,0:T(8,128)(2,1)S(1)} %get-tuple-element.32.refs_0_.refs_1_.s_ref, f32[1024,256]{1,0:T(8,128)S(1)} %get-tuple-element.45.refs_2_, ...), custom_call_target="tpu_custom_call", output_to_operand_aliasing={{0}: (0, {}), {1}: (2, {})} | custom-call | flops 2147483648 | bytes 4194304 | tf_op jit(solution)/shard_map/pallas_call | solution.py:175
  42.8 1.7 %shard_map.44 = (f32[1024,256]{1,0:T(8,128)S(1)}, bf16[1024,256]{1,0:T(8,128)(2,1)S(1)}) custom-call(f32[1024,256]{1,0:T(8,128)S(1)} %get-tuple-element.46.refs_0_, bf16[2048,256]{1,0:T(8,128)(2,1)S(1)} %get-tuple-element.32.refs_0_.refs_1_.s_ref, f32[1024,256]{1,0:T(8,128)S(1)} %get-tuple-element.47.refs_2_, ...), custom_call_target="tpu_custom_call", output_to_operand_aliasing={{0}: (0, {})} | custom-call | flops 1073741824 | bytes 4194304 | tf_op jit(solution)/shard_map/pallas_call | solution.py:175
  44.5 2.4 %collective-permute-start.10 = (bf16[1024,256]{1,0:T(8,128)(2,1)S(1)}, bf16[1024,256]{1,0:T(8,128)(2,1)S(1)}, u32[]{:S(2)}, u32[]{:S(2)}) collective-permute-start(bf16[1024,256]{1,0:T(8,128)(2,1)S(1)} %get-tuple-element.49), channel_id=1, source_target_pairs={{0,8},{1,9},{2,10},{3,11},{4,12},{5,13},{6,14},{7,15},{8,0},{9,1},... | collective-permute-start | bytes 1572872 | tf_op jit(solution)/shard_map/ppermute | solution.py:29
  46.9 2.9 %shard_map.38 = (f32[1024,256]{1,0:T(8,128)S(1)}, f32[1024,256]{1,0:T(8,128)S(1)}) custom-call(f32[1024,256]{1,0:T(8,128)S(1)} %get-tuple-element.33.refs_0_, bf16[2048,256]{1,0:T(8,128)(2,1)S(1)} %get-tuple-element.32.refs_0_.refs_1_.s_ref, f32[1024,256]{1,0:T(8,128)S(1)} %get-tuple-element.34.refs_2_, ...), custom_call_target="tpu_custom_call", output_to_operand_aliasing={{0}: (0, {}), {1}: (2, {})} | custom-call | flops 2147483648 | bytes 4194304 | tf_op jit(solution)/shard_map/pallas_call | solution.py:175
  49.8 2.9 %shard_map.39 = (f32[1024,256]{1,0:T(8,128)S(1)}, f32[1024,256]{1,0:T(8,128)S(1)}) custom-call(f32[1024,256]{1,0:T(8,128)S(1)} %get-tuple-element.35.refs_0_, bf16[2048,256]{1,0:T(8,128)(2,1)S(1)} %get-tuple-element.32.refs_0_.refs_1_.s_ref, f32[1024,256]{1,0:T(8,128)S(1)} %get-tuple-element.36.refs_2_, ...), custom_call_target="tpu_custom_call", output_to_operand_aliasing={{0}: (0, {}), {1}: (2, {})} | custom-call | flops 2147483648 | bytes 4194304 | tf_op jit(solution)/shard_map/pallas_call | solution.py:175
  52.8 1.7 %shard_map.40 = (f32[1024,256]{1,0:T(8,128)S(1)}, bf16[1024,256]{1,0:T(8,128)(2,1)S(1)}) custom-call(f32[1024,256]{1,0:T(8,128)S(1)} %get-tuple-element.37.refs_0_, bf16[2048,256]{1,0:T(8,128)(2,1)S(1)} %get-tuple-element.32.refs_0_.refs_1_.s_ref, f32[1024,256]{1,0:T(8,128)S(1)} %get-tuple-element.38.refs_2_, ...), custom_call_target="tpu_custom_call", output_to_operand_aliasing={{0}: (0, {})} | custom-call | flops 1073741824 | bytes 4194304 | tf_op jit(solution)/shard_map/pallas_call | solution.py:175
  57.1 5.4 %collective-permute-start.13 = (bf16[256,256]{1,0:T(8,128)(2,1)S(1)}, bf16[256,256]{1,0:T(8,128)(2,1)S(1)}, u32[]{:S(2)}, u32[]{:S(2)}) collective-permute-start(bf16[256,256]{1,0:T(8,128)(2,1)S(1)} %get-tuple-element.52), channel_id=1, source_target_pairs={{0,7},{1,4},{2,5},{3,6},{4,3},{5,0},{6,1},{7,2},{8,15},{9,12},{10,... | collective-permute-start | bytes 393224 | tf_op jit(solution)/shard_map/ppermute | solution.py:29
  65.1 1.4 %shard_map.41 = (bf16[256,256]{1,0:T(8,128)(2,1)S(1)}, bf16[256,256]{1,0:T(8,128)(2,1)S(1)}, bf16[256,256]{1,0:T(8,128)(2,1)S(1)}, f32[256,256]{1,0:T(8,128)S(1)}) custom-call(f32[1024,256]{1,0:T(8,128)S(1)} %get-tuple-element.39.start_ref, bf16[1024,256]{1,0:T(8,128)(2,1)S(1)} %collective-permute-done.7.handed_ref, ...), custom_call_target="tpu_custom_call" | custom-call | flops 1074790400 | bytes 4194304 | tf_op jit(solution)/shard_map/pallas_call | solution.py:204
  66.6 1.8 %collective-permute-start.15 = (bf16[256,256]{1,0:T(8,128)(2,1)S(1)}, bf16[256,256]{1,0:T(8,128)(2,1)S(1)}, u32[]{:S(2)}, u32[]{:S(2)}) collective-permute-start(bf16[256,256]{1,0:T(8,128)(2,1)S(1)} %get-tuple-element.54), channel_id=1, source_target_pairs={{0,1},{1,2},{2,3},{3,0},{4,5},{5,6},{6,7},{7,4},{8,9},{9,10},{10,1... | collective-permute-start | bytes 393224 | tf_op jit(solution)/shard_map/ppermute | solution.py:29
  71.8 3.0 %collective-permute-done.12.refs_1_ = bf16[256,256]{1,0:T(8,128)(2,1)S(1)} collective-permute-done((bf16[256,256]{1,0:T(8,128)(2,1)S(1)}, bf16[256,256]{1,0:T(8,128)(2,1)S(1)}, u32[]{:S(2)}, u32[]{:S(2)}) %collective-permute-start.12) | collective-permute-done | bytes 131104 | tf_op jit(solution)/shard_map/ppermute | solution.py:29
  74.8 2.7 %collective-permute-done.15.refs_4_ = bf16[256,256]{1,0:T(8,128)(2,1)S(1)} collective-permute-done((bf16[256,256]{1,0:T(8,128)(2,1)S(1)}, bf16[256,256]{1,0:T(8,128)(2,1)S(1)}, u32[]{:S(2)}, u32[]{:S(2)}) %collective-permute-start.15) | collective-permute-done | bytes 131104 | tf_op jit(solution)/shard_map/ppermute | solution.py:29
  77.5 2.8 %collective-permute-done.17.refs_6_ = bf16[256,256]{1,0:T(8,128)(2,1)S(1)} collective-permute-done((bf16[256,256]{1,0:T(8,128)(2,1)S(1)}, bf16[256,256]{1,0:T(8,128)(2,1)S(1)}, u32[]{:S(2)}, u32[]{:S(2)}) %collective-permute-start.17) | collective-permute-done | bytes 131104 | tf_op jit(solution)/shard_map/ppermute | solution.py:29
  (32 shorter events, 13.1 us)
Async XLA Ops:
  0.0 1.6 %copy-start = (f32[2048,256]{1,0:T(8,128)S(1)}, f32[2048,256]{1,0:T(8,128)}, u32[]{:S(2)}) copy-start(f32[2048,256]{1,0:T(8,128)} %s_hbm.1) | copy-start | bytes 6291460
  1.6 3.5 %copy-start.1 = (f32[512,256]{1,0:T(8,128)S(1)}, f32[512,256]{1,0:T(8,128)}, u32[]{:S(2)}) copy-start(f32[512,256]{1,0:T(8,128)} %p_hbm.1) | copy-start | bytes 1572868
  1.6 3.5 %copy-start.2 = (bf16[512,256]{1,0:T(8,128)(2,1)S(1)}, bf16[512,256]{1,0:T(8,128)(2,1)}, u32[]{:S(2)}) copy-start(bf16[512,256]{1,0:T(8,128)(2,1)} %i_hbm.1) | copy-start | bytes 786436
  3.6 20.6 %collective-permute-start = (bf16[2048,256]{1,0:T(8,128)(2,1)S(1)}, bf16[2048,256]{1,0:T(8,128)(2,1)S(1)}, u32[]{:S(2)}, u32[]{:S(2)}) collective-permute-start(bf16[2048,256]{1,0:T(8,128)(2,1)S(1)} %get-tuple-element.32.refs_0_.refs_1_.s_ref), channel_id=1, source_target_pairs={{0,8},{1,9},{2,10},{3,11},{4,12},{5,13},{6,14},{7,15},{8,0},{9,1},... | collective-permute-start | bytes 3145736 | tf_op jit(solution)/shard_map/ppermute | solution.py:29
  5.4 8.8 %collective-permute-start.1 = (bf16[512,512]{1,0:T(8,128)(2,1)S(1)}, bf16[512,512]{1,0:T(8,128)(2,1)S(1)}, u32[]{:S(2)}, u32[]{:S(2)}) collective-permute-start(bf16[512,512]{1,0:T(8,128)(2,1)S(1)} %pack_data.1.refs_2_), channel_id=1, source_target_pairs={{0,16},{1,17},{2,18},{3,19},{4,20},{5,21},{6,22},{7,23},{8,56},{9,... | collective-permute-start | bytes 1572872 | tf_op jit(solution)/shard_map/ppermute | solution.py:29
  8.1 14.7 %collective-permute-start.3 = (bf16[512,512]{1,0:T(8,128)(2,1)S(1)}, bf16[512,512]{1,0:T(8,128)(2,1)S(1)}, u32[]{:S(2)}, u32[]{:S(2)}) collective-permute-start(bf16[512,512]{1,0:T(8,128)(2,1)S(1)} %pack_data.1.refs_2_), channel_id=1, source_target_pairs={{0,68},{1,69},{2,70},{3,71},{4,64},{5,65},{6,66},{7,67},{8,76},{9,... | collective-permute-start | bytes 1572872 | tf_op jit(solution)/shard_map/ppermute | solution.py:29
  14.2 14.9 %collective-permute-start.4 = (bf16[512,512]{1,0:T(8,128)(2,1)S(1)}, bf16[512,512]{1,0:T(8,128)(2,1)S(1)}, u32[]{:S(2)}, u32[]{:S(2)}) collective-permute-start(bf16[512,512]{1,0:T(8,128)(2,1)S(1)} %collective-permute-done.1.refs_3_), channel_id=1, source_target_pairs={{0,16},{1,17},{2,18},{3,19},{4,20},{5,21},{6,22},{7,23},{8,56},{9,... | collective-permute-start | bytes 1572872 | tf_op jit(solution)/shard_map/ppermute | solution.py:29
  17.6 15.2 %collective-permute-start.2 = (bf16[512,512]{1,0:T(8,128)(2,1)S(1)}, bf16[512,512]{1,0:T(8,128)(2,1)S(1)}, u32[]{:S(2)}, u32[]{:S(2)}) collective-permute-start(bf16[512,512]{1,0:T(8,128)(2,1)S(1)} %pack_data.1.refs_2_), channel_id=1, source_target_pairs={{0,48},{1,49},{2,50},{3,51},{4,52},{5,53},{6,54},{7,55},{8,24},{9,... | collective-permute-start | bytes 1572872 | tf_op jit(solution)/shard_map/ppermute | solution.py:29
  22.8 16.1 %collective-permute-start.5 = (bf16[512,512]{1,0:T(8,128)(2,1)S(1)}, bf16[512,512]{1,0:T(8,128)(2,1)S(1)}, u32[]{:S(2)}, u32[]{:S(2)}) collective-permute-start(bf16[512,512]{1,0:T(8,128)(2,1)S(1)} %collective-permute-done.3.refs_5_), channel_id=1, source_target_pairs={{0,16},{1,17},{2,18},{3,19},{4,20},{5,21},{6,22},{7,23},{8,56},{9,... | collective-permute-start | bytes 1572872 | tf_op jit(solution)/shard_map/ppermute | solution.py:29
  23.6 19.2 %collective-permute-start.6 = (bf16[512,512]{1,0:T(8,128)(2,1)S(1)}, bf16[512,512]{1,0:T(8,128)(2,1)S(1)}, u32[]{:S(2)}, u32[]{:S(2)}) collective-permute-start(bf16[512,512]{1,0:T(8,128)(2,1)S(1)} %collective-permute-done.3.refs_5_), channel_id=1, source_target_pairs={{0,48},{1,49},{2,50},{3,51},{4,52},{5,53},{6,54},{7,55},{8,24},{9,... | collective-permute-start | bytes 1572872 | tf_op jit(solution)/shard_map/ppermute | solution.py:29
  29.2 23.5 %collective-permute-start.8 = (bf16[512,512]{1,0:T(8,128)(2,1)S(1)}, bf16[512,512]{1,0:T(8,128)(2,1)S(1)}, u32[]{:S(2)}, u32[]{:S(2)}) collective-permute-start(bf16[512,512]{1,0:T(8,128)(2,1)S(1)} %collective-permute-done.4.refs_4_), channel_id=1, source_target_pairs={{0,68},{1,69},{2,70},{3,71},{4,64},{5,65},{6,66},{7,67},{8,76},{9,... | collective-permute-start | bytes 1572872 | tf_op jit(solution)/shard_map/ppermute | solution.py:29
  44.5 11.9 %collective-permute-start.10 = (bf16[1024,256]{1,0:T(8,128)(2,1)S(1)}, bf16[1024,256]{1,0:T(8,128)(2,1)S(1)}, u32[]{:S(2)}, u32[]{:S(2)}) collective-permute-start(bf16[1024,256]{1,0:T(8,128)(2,1)S(1)} %get-tuple-element.49), channel_id=1, source_target_pairs={{0,8},{1,9},{2,10},{3,11},{4,12},{5,13},{6,14},{7,15},{8,0},{9,1},... | collective-permute-start | bytes 1572872 | tf_op jit(solution)/shard_map/ppermute | solution.py:29
  52.7 3.8 %collective-permute-start.9 = (bf16[512,512]{1,0:T(8,128)(2,1)S(1)}, bf16[512,512]{1,0:T(8,128)(2,1)S(1)}, u32[]{:S(2)}, u32[]{:S(2)}) collective-permute-start(bf16[512,512]{1,0:T(8,128)(2,1)S(1)} %collective-permute-done.8.refs_0_.refs_2_), channel_id=1, source_target_pairs={{0,8},{1,9},{2,10},{3,11},{4,12},{5,13},{6,14},{7,15},{8,0},{9,1},... | collective-permute-start | bytes 1572872 | tf_op jit(solution)/shard_map/ppermute | solution.py:29
  54.5 10.6 %collective-permute-start.7 = (bf16[1024,256]{1,0:T(8,128)(2,1)S(1)}, bf16[1024,256]{1,0:T(8,128)(2,1)S(1)}, u32[]{:S(2)}, u32[]{:S(2)}) collective-permute-start(bf16[1024,256]{1,0:T(8,128)(2,1)S(1)} %get-tuple-element.40), channel_id=1, source_target_pairs={{0,8},{1,9},{2,10},{3,11},{4,12},{5,13},{6,14},{7,15},{8,0},{9,1},... | collective-permute-start | bytes 1572872 | tf_op jit(solution)/shard_map/ppermute | solution.py:29
  57.1 11.2 %collective-permute-start.13 = (bf16[256,256]{1,0:T(8,128)(2,1)S(1)}, bf16[256,256]{1,0:T(8,128)(2,1)S(1)}, u32[]{:S(2)}, u32[]{:S(2)}) collective-permute-start(bf16[256,256]{1,0:T(8,128)(2,1)S(1)} %get-tuple-element.52), channel_id=1, source_target_pairs={{0,7},{1,4},{2,5},{3,6},{4,3},{5,0},{6,1},{7,2},{8,15},{9,12},{10,... | collective-permute-start | bytes 393224 | tf_op jit(solution)/shard_map/ppermute | solution.py:29
  62.5 6.8 %collective-permute-start.14 = (bf16[256,256]{1,0:T(8,128)(2,1)S(1)}, bf16[256,256]{1,0:T(8,128)(2,1)S(1)}, u32[]{:S(2)}, u32[]{:S(2)}) collective-permute-start(bf16[256,256]{1,0:T(8,128)(2,1)S(1)} %get-tuple-element.53), channel_id=1, source_target_pairs={{0,4},{1,5},{2,6},{3,7},{4,0},{5,1},{6,2},{7,3},{8,12},{9,13},{10,... | collective-permute-start | bytes 393224 | tf_op jit(solution)/shard_map/ppermute | solution.py:29
  63.2 8.6 %collective-permute-start.11 = (bf16[256,256]{1,0:T(8,128)(2,1)S(1)}, bf16[256,256]{1,0:T(8,128)(2,1)S(1)}, u32[]{:S(2)}, u32[]{:S(2)}) collective-permute-start(bf16[256,256]{1,0:T(8,128)(2,1)S(1)} %get-tuple-element.50), channel_id=1, source_target_pairs={{0,6},{1,7},{2,4},{3,5},{4,2},{5,3},{6,0},{7,1},{8,14},{9,15},{10,... | collective-permute-start | bytes 393224 | tf_op jit(solution)/shard_map/ppermute | solution.py:29
  64.1 10.7 %collective-permute-start.12 = (bf16[256,256]{1,0:T(8,128)(2,1)S(1)}, bf16[256,256]{1,0:T(8,128)(2,1)S(1)}, u32[]{:S(2)}, u32[]{:S(2)}) collective-permute-start(bf16[256,256]{1,0:T(8,128)(2,1)S(1)} %get-tuple-element.51), channel_id=1, source_target_pairs={{0,5},{1,6},{2,7},{3,4},{4,1},{5,2},{6,3},{7,0},{8,13},{9,14},{10,... | collective-permute-start | bytes 393224 | tf_op jit(solution)/shard_map/ppermute | solution.py:29
  66.6 11.0 %collective-permute-start.15 = (bf16[256,256]{1,0:T(8,128)(2,1)S(1)}, bf16[256,256]{1,0:T(8,128)(2,1)S(1)}, u32[]{:S(2)}, u32[]{:S(2)}) collective-permute-start(bf16[256,256]{1,0:T(8,128)(2,1)S(1)} %get-tuple-element.54), channel_id=1, source_target_pairs={{0,1},{1,2},{2,3},{3,0},{4,5},{5,6},{6,7},{7,4},{8,9},{9,10},{10,1... | collective-permute-start | bytes 393224 | tf_op jit(solution)/shard_map/ppermute | solution.py:29
  68.4 9.2 %collective-permute-start.16 = (bf16[256,256]{1,0:T(8,128)(2,1)S(1)}, bf16[256,256]{1,0:T(8,128)(2,1)S(1)}, u32[]{:S(2)}, u32[]{:S(2)}) collective-permute-start(bf16[256,256]{1,0:T(8,128)(2,1)S(1)} %get-tuple-element.55), channel_id=1, source_target_pairs={{0,3},{1,0},{2,1},{3,2},{4,7},{5,4},{6,5},{7,6},{8,11},{9,8},{10,9... | collective-permute-start | bytes 393224 | tf_op jit(solution)/shard_map/ppermute | solution.py:29
  69.3 11.0 %collective-permute-start.17 = (bf16[256,256]{1,0:T(8,128)(2,1)S(1)}, bf16[256,256]{1,0:T(8,128)(2,1)S(1)}, u32[]{:S(2)}, u32[]{:S(2)}) collective-permute-start(bf16[256,256]{1,0:T(8,128)(2,1)S(1)} %get-tuple-element.56), channel_id=1, source_target_pairs={{0,2},{1,3},{2,0},{3,1},{4,6},{5,7},{6,4},{7,5},{8,10},{9,11},{10,... | collective-permute-start | bytes 393224 | tf_op jit(solution)/shard_map/ppermute | solution.py:29
where the time goes:
time: 81.3 us; the launch traced here: 81.2 us
  starting transfers between devices  28.9 us (36%)
  Pallas kernels  27.3 us (34%)
  waiting for transfers between devices  23.3 us (29%)
  local copies, waits for them, and re-layouts  1.6 us (2%)
    ppermute x18, starting transfers between devices, sent(): lax.ppermute(value, AXES, [(i, index(*to(*place(i)))) for i in range(128)])  28.9 us
    ppermute x18, waiting for transfers between devices, sent(): lax.ppermute(value, AXES, [(i, index(*to(*place(i)))) for i in range(128)])  23.3 us
    pallas_call x8, Pallas kernels, add_chunks(): pl.pallas_call(body, out_shape=[jax.ShapeDtypeStruct((half, members), kin...  21.3 us
    pallas_call x3, Pallas kernels, last_chunks(): pl.pallas_call(body, out_shape=[jax.ShapeDtypeStruct((own, members), jnp....  2.84 us
    pallas_call x1, Pallas kernels, prepare_state(): pl.pallas_call(body, out_shape=(jax.ShapeDtypeStruct((rows, members), jnp...  2.01 us
  transfers between devices with their start and end apart: 18, of which 9 were waited for; matrix products, arithmetic and copies ran while one was open for 0% of the time, Pallas kernels for 30%

commit v1 on v0

--- a/solution.py
+++ b/solution.py
@@ -58,26 +58,41 @@
 
 def pack_data(predicted, innovations):
     rows, members = predicted.shape
-
-    def body(p_hbm, i_hbm, o_ref, p_ref, sems):
-        values = pltpu.make_async_copy(p_hbm, p_ref, sems.at[0])
-        copied = pltpu.make_async_copy(i_hbm, o_ref.at[:, members:], sems.at[1])
-        values.start()
-        copied.start()
-        values.wait()
-        o_ref[:, 0:members] = standard(p_ref[...])[0]
-        copied.wait()
+    pieces = 4
+    step = rows // pieces
+
+    def body(p_hbm, i_hbm, o_ref, p_ref, i_ref, sems):
+        copies = []
+        for k in range(pieces):
+            part = pl.ds(k * step, step)
+            copies.append(pltpu.make_async_copy(p_hbm.at[part, :], p_ref.at[part, :], sems.at[k]))
+        copies.append(pltpu.make_async_copy(i_hbm, i_ref, sems.at[pieces]))
+        for copy in copies:
+            copy.start()
+        for k in range(pieces):
+            copies[k].wait()
+            part = pl.ds(k * step, step)
+            o_ref[part, 0:members] = standard(p_ref[part, :])[0]
+        copies[pieces].wait()
+        o_ref[:, members:] = i_ref[...]
 
     return pl.pallas_call(
         body,
         out_shape=jax.ShapeDtypeStruct((rows, 2 * members), jnp.bfloat16),
         in_specs=[HBM] * 2,
         out_specs=VMEM,
-        scratch_shapes=[pltpu.VMEM((rows, members), jnp.float32), pltpu.SemaphoreType.DMA((2,))],
+        scratch_shapes=[
+            pltpu.VMEM((rows, members), jnp.float32),
+            pltpu.VMEM((rows, members), jnp.bfloat16),
+            pltpu.SemaphoreType.DMA((pieces + 1,)),
+        ],
         compiler_params=pltpu.CompilerParams(vmem_limit_bytes=LIMIT),
         cost_estimate=cost(1 << 20, 1 << 20),
         name="pack_data",
-    )(predicted, innovations)
+    )(
+        pltpu.with_memory_space_constraint(predicted, pltpu.HBM),
+        pltpu.with_memory_space_constraint(innovations, pltpu.HBM),
+    )
 
 
 def prepare_state(state, own):
@@ -132,9 +147,10 @@
     return total
 
 
-def half_start(far, half):
+def half_start(first, mine, half):
+    core = lax.rem(lax.axis_index("state"), 2)
     lo = lax.axis_index("dp") // 4
-    return (1 - lo if far else lo) * half
+    return lax.rem(lo + core + (1 if first == mine else 0), 2) * half
 
 
 def add_chunks(parts, chunks, sent_kinds=(), tile=1024):
@@ -142,13 +158,13 @@
     half = parts[0][1].shape[0] // 2
     kinds = [jnp.bfloat16 if k in sent_kinds else jnp.float32 for k in range(len(parts))]
     operands, aliases, places = [], {}, []
-    for k, (start, state, far) in enumerate(parts):
+    for k, (start, state, *which) in enumerate(parts):
         if start is not None and kinds[k] == jnp.float32:
             aliases[len(operands)] = k
         if start is not None:
             operands.append(start)
         states = [i for i, o in enumerate(operands) if o is state]
-        places.append((None if start is None else len(operands) - 1, len(operands) if not states else states[0], far))
+        places.append((None if start is None else len(operands) - 1, len(operands) if not states else states[0], which))
         if not states:
             operands.append(state)
     count = len(operands)
@@ -156,8 +172,8 @@
 
     def body(*refs):
         x_refs, o_refs = refs[count : len(operands)], refs[len(operands) :]
-        for (start_at, state_at, far), o_ref in zip(places, o_refs):
-            base = half_start(far, half)
+        for (start_at, state_at, which), o_ref in zip(places, o_refs):
+            base = half_start(*which, half)
 
             def step(i, _):
                 there = pl.ds(pl.multiple_of(i * tile, tile), tile)
@@ -183,52 +199,55 @@
     )(*operands)
 
 
-def last_chunks(running, handed, state, chunks, own, far, steps):
+def last_chunks(running, handed, state, chunks, own, first, steps, kept=None):
     members = running.shape[1]
     count = len(chunks)
 
     def body(start_ref, handed_ref, s_ref, *refs):
-        x_refs, o_refs = refs[:count], refs[count:]
+        x_refs, o_refs = refs[:count], refs[count + (kept is not None) :]
         z = lax.rem(lax.axis_index("dp"), 4)
-        base = half_start(far, running.shape[0])
+        base = half_start(first, True, running.shape[0])
         rows = [pl.multiple_of(lax.rem(z + k, 4) * own, own) for k in steps]
         totals = [start_ref[pl.ds(r, own), :] + handed_ref[pl.ds(r, own), :].astype(jnp.float32) for r in rows]
-        if count:
-            state_rows = jnp.concatenate([s_ref[pl.ds(base + r, own), :] for r in rows], axis=0)
-            total = tile_sum(state_rows, x_refs, jnp.concatenate(totals, axis=0), members)
-            totals = [total[j * own : (j + 1) * own, :] for j in range(len(steps))]
-        for total, o_ref in zip(totals, o_refs):
-            o_ref[...] = total.astype(o_ref.dtype)
-
-    operands = [running, handed, state, *chunks]
-    return pl.pallas_call(
-        body,
-        out_shape=[
-            jax.ShapeDtypeStruct((own, members), jnp.bfloat16 if far or k else jnp.float32) for k in steps
-        ],
+        state_rows = jnp.concatenate([s_ref[pl.ds(base + r, own), :] for r in rows], axis=0)
+        total = tile_sum(state_rows, x_refs, jnp.concatenate(totals, axis=0), members)
+        blocks = [total[j * own : (j + 1) * own, :] for j in range(len(steps))]
+        if kept is not None:
+            upper = jnp.full(blocks[-1].shape, lax.rem(lax.axis_index("state"), 2)) == 1
+            mine, other = blocks[-1], refs[count][...]
+            blocks[-1:] = [jnp.where(upper, mine, other), jnp.where(upper, other, mine)]
+        for block, o_ref in zip(blocks, o_refs):
+            o_ref[...] = block.astype(o_ref.dtype)
+
+    operands = [running, handed, state, *chunks] + ([] if kept is None else [kept])
+    kinds = [jnp.float32 if k == 0 and kept is None else jnp.bfloat16 for k in steps]
+    kinds += [] if kept is None else [jnp.float32]
+    return pl.pallas_call(
+        body,
+        out_shape=[jax.ShapeDtypeStruct((own, members), kind) for kind in kinds],
         in_specs=[VMEM] * len(operands),
-        out_specs=[VMEM] * len(steps),
+        out_specs=[VMEM] * len(kinds),
         compiler_params=pltpu.CompilerParams(vmem_limit_bytes=LIMIT),
         cost_estimate=cost(4 * len(steps) * own * members * 512 * count + (1 << 20), 1 << 22),
     )(*operands)
 
 
-def finish(spread, own_block, blocks):
-    def body(w_ref, f_ref, *refs):
-        total = f_ref[...]
-        for ref in refs[:-1]:
+def finish(spread, blocks):
+    def body(w_ref, *refs):
+        total = refs[0][...].astype(jnp.float32)
+        for ref in refs[1:-1]:
             total = total + ref[...].astype(jnp.float32)
         refs[-1][...] = w_ref[...] * total
 
     return pl.pallas_call(
         body,
-        out_shape=jax.ShapeDtypeStruct(own_block.shape, jnp.float32),
-        in_specs=[VMEM] * (2 + len(blocks)),
+        out_shape=jax.ShapeDtypeStruct(spread.shape, jnp.float32),
+        in_specs=[VMEM] * (1 + len(blocks)),
         out_specs=VMEM,
         compiler_params=pltpu.CompilerParams(vmem_limit_bytes=LIMIT),
         cost_estimate=cost(1 << 20, 1 << 20),
         name="finish",
-    )(spread, own_block, *blocks)
+    )(spread, *blocks)
 
 
 def update(state_ensemble, predicted_data, innovations):
@@ -243,27 +262,30 @@
     q1a = sent(y0, x_turn)
     q1b = sent(y0, x_back)
     y2 = sent(p2, y_across)
-    early = [(None, s, True), (None, t, True), (None, s, False), (None, t, False)]
-    fs, ft, ns, nt = add_chunks(early, [x0, p1a])
-    ns, nt = add_chunks([(ns, s, False), (nt, t, False)], [p1b, y0])
-    fs, ft = add_chunks([(fs, s, True), (ft, t, True)], [p1b, y0])
-    fs, ft = add_chunks([(fs, s, True), (ft, t, True)], [p2, q1a])
-    ns, nt = add_chunks([(ns, s, False), (nt, t, False)], [p2, q1a])
-    fs, ft = add_chunks([(fs, s, True), (ft, t, True)], [q1b], sent_kinds=(1,))
+
+    def added(sums, chunks):
+        rows = ((s, True, True), (t, True, False), (s, False, True), (t, False, False))
+        return add_chunks([(total, *row) for total, row in zip(sums, rows)], chunks)
+
+    sums = added([None] * 4, [x0, p1a])
+    sums = added(sums, [y0])
+    sums = added(sums, [p1b, p2])
+    fs, ft, ns, nt = added(sums, [q1a])
+    fs, ft = add_chunks([(fs, s, True, True), (ft, t, True, False)], [q1b], sent_kinds=(1,))
     fh = sent(ft, other_core)
-    ns, nt = add_chunks([(ns, s, False), (nt, t, False)], [q1b], sent_kinds=(1,))
+    ns, nt = add_chunks([(ns, s, False, True), (nt, t, False, False)], [q1b], sent_kinds=(1,))
     nh = sent(nt, other_core)
     y2s = sent(y2, other_core)
-    (fs,) = add_chunks([(fs, s, True)], [y2])
+    (fs,) = add_chunks([(fs, s, True, True)], [y2])
     blocks = {}
-    blocks[1, 2], blocks[1, 1] = last_chunks(fs, fh, s, [y2s], own, True, (2, 1))
-    blocks[1, 3], blocks[1, 0] = last_chunks(fs, fh, s, [y2s], own, True, (3, 0))
-    near = last_chunks(ns, nh, s, [y2, y2s], own, False, (1, 3, 2, 0))
-    blocks[0, 1], blocks[0, 3], blocks[0, 2], mine = near
-    arrived = []
-    for (across, k), block in blocks.items():
-        arrived.append(sent(block, lambda x, y, z, core: (x, y ^ across, z + k, core)))
-    return finish(spread, mine, arrived)
+    blocks[0, 2], blocks[0, 1] = last_chunks(fs, fh, s, [y2s], own, True, (2, 1))
+    blocks[0, 3], kept = last_chunks(fs, fh, s, [y2s], own, True, (3, 0))
+    second = last_chunks(ns, nh, s, [y2, y2s], own, False, (2, 1, 3, 0), kept)
+    blocks[1, 2], blocks[1, 1], blocks[1, 3], across, mine = second
+    arrived = [mine, sent(across, lambda x, y, z, core: (x, y ^ 1, z, core))]
+    for (later, k), block in blocks.items():
+        arrived.append(sent(block, lambda x, y, z, core: (x, y ^ int(core == later), z + k, core)))
+    return finish(spread, arrived)
 
 
 def solution(mesh):

time: 81.3 us -> 75.6 us (0.930); the launches traced: 81.2 us -> 74.3 us
  waiting for transfers between devices: 23.3 us -> 13.8 us
  Pallas kernels: 27.3 us -> 28.8 us
  starting transfers between devices: 28.9 us -> 29.9 us
    ppermute x18, waiting for transfers between devices: 23.3 us -> 13.8 us  [sent(): lax.ppermute(value, AXES, [(i, index(*to(*place(i)))) for i in range(128)])]
    pallas_call x1, Pallas kernels: 0.35 us -> 1.76 us  [pack_data(): pl.pallas_call(body, out_shape=jax.ShapeDtypeStruct((rows, 2 * members),...]
    ppermute x18, starting transfers between devices: 28.9 us -> 29.9 us  [sent(): lax.ppermute(value, AXES, [(i, index(*to(*place(i)))) for i in range(128)])]
    pallas_call x8 -> x7, Pallas kernels: 21.3 us -> 21.4 us  [add_chunks(): pl.pallas_call(body, out_shape=[jax.ShapeDtypeStruct((half, members), kin...]
  transfers between devices with their start and end apart: 18 -> 18, of which waited for: 9 -> 5; matrix products, arithmetic and copies ran while one was open for 0% -> 0% of each run, Pallas kernels for 30% -> 33%
where the time goes in v1:
time: 75.6 us; the launch traced here: 74.3 us
  starting transfers between devices  29.9 us (40%)
  Pallas kernels  28.8 us (38%)
  waiting for transfers between devices  13.8 us (18%)
  local copies, waits for them, and re-layouts  1.59 us (2%)
    ppermute x18, starting transfers between devices, sent(): lax.ppermute(value, AXES, [(i, index(*to(*place(i)))) for i in range(128)])  29.9 us
    pallas_call x7, Pallas kernels, add_chunks(): pl.pallas_call(body, out_shape=[jax.ShapeDtypeStruct((half, members), kin...  21.4 us
    ppermute x18, waiting for transfers between devices, sent(): lax.ppermute(value, AXES, [(i, index(*to(*place(i)))) for i in range(128)])  13.8 us
    pallas_call x3, Pallas kernels, last_chunks(): pl.pallas_call(body, out_shape=[jax.ShapeDtypeStruct((own, members), kind...  2.85 us
    pallas_call x1, Pallas kernels, prepare_state(): pl.pallas_call(body, out_shape=(jax.ShapeDtypeStruct((rows, members), jnp...  2.01 us
    pallas_call x1, Pallas kernels, pack_data(): pl.pallas_call(body, out_shape=jax.ShapeDtypeStruct((rows, 2 * members),...  1.76 us
    unnamed x2, local copies, waits for them, and re-layouts  1.59 us
  transfers between devices with their start and end apart: 18, of which 5 were waited for; matrix products, arithmetic and copies ran while one was open for 0% of the time, Pallas kernels for 33%

profile of v1, /device:TPU:1, one launch (start us, length us, event | category | flops | bytes accessed | tf_op | source)
XLA Modules:
  0.0 74.3 jit_solution(17650090882316089853)
XLA Ops:
  0.0 1.8 %pack_data.1.refs_2_ = bf16[512,512]{1,0:T(8,128)(2,1)S(1)} custom-call(f32[512,256]{1,0:T(8,128)} %p_hbm.1, bf16[512,256]{1,0:T(8,128)(2,1)} %i_hbm.1), custom_call_target="tpu_custom_call" | custom-call | flops 1048576 | bytes 1048576 | tf_op jit(solution)/shard_map/pack_data/pallas_call | solution.py:79
  1.8 3.4 %collective-permute-start.1 = (bf16[512,512]{1,0:T(8,128)(2,1)S(1)}, bf16[512,512]{1,0:T(8,128)(2,1)S(1)}, u32[]{:S(2)}, u32[]{:S(2)}) collective-permute-start(bf16[512,512]{1,0:T(8,128)(2,1)S(1)} %pack_data.1.refs_2_), channel_id=1, source_target_pairs={{0,16},{1,17},{2,18},{3,19},{4,20},{5,21},{6,22},{7,23},{8,56},{9,... | collective-permute-start | bytes 1572872 | tf_op jit(solution)/shard_map/ppermute | solution.py:29
  5.1 1.6 %copy-done = f32[2048,256]{1,0:T(8,128)S(1)} copy-done((f32[2048,256]{1,0:T(8,128)S(1)}, f32[2048,256]{1,0:T(8,128)}, u32[]{:S(2)}) %copy-start) | copy-done | bytes 2097176
  6.7 2.0 %prepare_state.1 = (bf16[2048,256]{1,0:T(8,128)(2,1)S(1)}, f32[256,256]{1,0:T(8,128)S(1)}) custom-call(f32[2048,256]{1,0:T(8,128)S(1)} %copy-done), custom_call_target="tpu_custom_call" | custom-call | flops 16777216 | bytes 4194304 | tf_op jit(solution)/shard_map/prepare_state/pallas_call | solution.py:119
  8.8 2.8 %collective-permute-start.2 = (bf16[512,512]{1,0:T(8,128)(2,1)S(1)}, bf16[512,512]{1,0:T(8,128)(2,1)S(1)}, u32[]{:S(2)}, u32[]{:S(2)}) collective-permute-start(bf16[512,512]{1,0:T(8,128)(2,1)S(1)} %pack_data.1.refs_2_), channel_id=1, source_target_pairs={{0,68},{1,69},{2,70},{3,71},{4,64},{5,65},{6,66},{7,67},{8,76},{9,... | collective-permute-start | bytes 1572872 | tf_op jit(solution)/shard_map/ppermute | solution.py:29
  11.7 3.0 %collective-permute-start.4 = (bf16[512,512]{1,0:T(8,128)(2,1)S(1)}, bf16[512,512]{1,0:T(8,128)(2,1)S(1)}, u32[]{:S(2)}, u32[]{:S(2)}) collective-permute-start(bf16[512,512]{1,0:T(8,128)(2,1)S(1)} %collective-permute-done.1.refs_3_), channel_id=1, source_target_pairs={{0,16},{1,17},{2,18},{3,19},{4,20},{5,21},{6,22},{7,23},{8,56},{9,... | collective-permute-start | bytes 1572872 | tf_op jit(solution)/shard_map/ppermute | solution.py:29
  14.7 8.6 %collective-permute-done.2.refs_6_ = bf16[512,512]{1,0:T(8,128)(2,1)S(1)} collective-permute-done((bf16[512,512]{1,0:T(8,128)(2,1)S(1)}, bf16[512,512]{1,0:T(8,128)(2,1)S(1)}, u32[]{:S(2)}, u32[]{:S(2)}) %collective-permute-start.2) | collective-permute-done | bytes 524320 | tf_op jit(solution)/shard_map/ppermute | solution.py:29
  23.3 1.5 %collective-permute-start.5 = (bf16[512,512]{1,0:T(8,128)(2,1)S(1)}, bf16[512,512]{1,0:T(8,128)(2,1)S(1)}, u32[]{:S(2)}, u32[]{:S(2)}) collective-permute-start(bf16[512,512]{1,0:T(8,128)(2,1)S(1)} %collective-permute-done.2.refs_6_), channel_id=1, source_target_pairs={{0,16},{1,17},{2,18},{3,19},{4,20},{5,21},{6,22},{7,23},{8,56},{9,... | collective-permute-start | bytes 1572872 | tf_op jit(solution)/shard_map/ppermute | solution.py:29
  24.8 2.6 %collective-permute-start.8 = (bf16[512,512]{1,0:T(8,128)(2,1)S(1)}, bf16[512,512]{1,0:T(8,128)(2,1)S(1)}, u32[]{:S(2)}, u32[]{:S(2)}) collective-permute-start(bf16[512,512]{1,0:T(8,128)(2,1)S(1)} %collective-permute-done.4.refs_7_), channel_id=1, source_target_pairs={{0,68},{1,69},{2,70},{3,71},{4,64},{5,65},{6,66},{7,67},{8,76},{9,... | collective-permute-start | bytes 1572872 | tf_op jit(solution)/shard_map/ppermute | solution.py:29
  27.4 4.9 %shard_map.37 = (f32[1024,256]{1,0:T(8,128)S(1)}, f32[1024,256]{1,0:T(8,128)S(1)}, f32[1024,256]{1,0:T(8,128)S(1)}, f32[1024,256]{1,0:T(8,128)S(1)}) custom-call(bf16[2048,256]{1,0:T(8,128)(2,1)S(1)} %get-tuple-element.37.refs_0_.refs_1_.s_ref, bf16[2048,256]{1,0:T(8,128)(2,1)S(1)} %collective-permute-done.refs_1_.refs_3_, ...), custom_call_target="tpu_custom_call" | custom-call | flops 4294967296 | bytes 4194304 | tf_op jit(solution)/shard_map/pallas_call | solution.py:191
  32.3 3.1 %shard_map.38 = (f32[1024,256]{1,0:T(8,128)S(1)}, f32[1024,256]{1,0:T(8,128)S(1)}, f32[1024,256]{1,0:T(8,128)S(1)}, f32[1024,256]{1,0:T(8,128)S(1)}) custom-call(f32[1024,256]{1,0:T(8,128)S(1)} %get-tuple-element.38.refs_0_, ...), custom_call_target="tpu_custom_call", output_to_operand_aliasing={{0}: (0, {}), {1}: (2, {}), {2}: (4, {}), {3}: (5, {})} | custom-call | flops 2147483648 | bytes 4194304 | tf_op jit(solution)/shard_map/pallas_call | solution.py:191
  35.4 5.5 %shard_map.39 = (f32[1024,256]{1,0:T(8,128)S(1)}, f32[1024,256]{1,0:T(8,128)S(1)}, f32[1024,256]{1,0:T(8,128)S(1)}, f32[1024,256]{1,0:T(8,128)S(1)}) custom-call(f32[1024,256]{1,0:T(8,128)S(1)} %get-tuple-element.42.refs_0_, ...), custom_call_target="tpu_custom_call", output_to_operand_aliasing={{0}: (0, {}), {1}: (2, {}), {2}: (4, {}), {3}: (5, {})} | custom-call | flops 4294967296 | bytes 4194304 | tf_op jit(solution)/shard_map/pallas_call | solution.py:191
  40.9 3.1 %shard_map.40 = (f32[1024,256]{1,0:T(8,128)S(1)}, f32[1024,256]{1,0:T(8,128)S(1)}, f32[1024,256]{1,0:T(8,128)S(1)}, f32[1024,256]{1,0:T(8,128)S(1)}) custom-call(f32[1024,256]{1,0:T(8,128)S(1)} %get-tuple-element.46.refs_0_, ...), custom_call_target="tpu_custom_call", output_to_operand_aliasing={{0}: (0, {}), {1}: (2, {}), {2}: (4, {}), {3}: (5, {})} | custom-call | flops 2147483648 | bytes 4194304 | tf_op jit(solution)/shard_map/pallas_call | solution.py:191
  44.0 1.7 %shard_map.42 = (f32[1024,256]{1,0:T(8,128)S(1)}, bf16[1024,256]{1,0:T(8,128)(2,1)S(1)}) custom-call(f32[1024,256]{1,0:T(8,128)S(1)} %get-tuple-element.54.refs_0_, bf16[2048,256]{1,0:T(8,128)(2,1)S(1)} %get-tuple-element.37.refs_0_.refs_1_.s_ref, f32[1024,256]{1,0:T(8,128)S(1)} %get-tuple-element.55.refs_2_, ...), custom_call_target="tpu_custom_call", output_to_operand_aliasing={{0}: (0, {})} | custom-call | flops 1073741824 | bytes 4194304 | tf_op jit(solution)/shard_map/pallas_call | solution.py:191
  45.8 4.9 %collective-permute-start.10 = (bf16[1024,256]{1,0:T(8,128)(2,1)S(1)}, bf16[1024,256]{1,0:T(8,128)(2,1)S(1)}, u32[]{:S(2)}, u32[]{:S(2)}) collective-permute-start(bf16[1024,256]{1,0:T(8,128)(2,1)S(1)} %get-tuple-element.57), channel_id=1, source_target_pairs={{0,8},{1,9},{2,10},{3,11},{4,12},{5,13},{6,14},{7,15},{8,0},{9,1},... | collective-permute-start | bytes 1572872 | tf_op jit(solution)/shard_map/ppermute | solution.py:29
  50.8 1.7 %shard_map.41 = (f32[1024,256]{1,0:T(8,128)S(1)}, bf16[1024,256]{1,0:T(8,128)(2,1)S(1)}) custom-call(f32[1024,256]{1,0:T(8,128)S(1)} %get-tuple-element.50.refs_0_, bf16[2048,256]{1,0:T(8,128)(2,1)S(1)} %get-tuple-element.37.refs_0_.refs_1_.s_ref, f32[1024,256]{1,0:T(8,128)S(1)} %get-tuple-element.51.refs_2_, ...), custom_call_target="tpu_custom_call", output_to_operand_aliasing={{0}: (0, {})} | custom-call | flops 1073741824 | bytes 4194304 | tf_op jit(solution)/shard_map/pallas_call | solution.py:191
  53.1 1.3 %shard_map.43.start_ref = f32[1024,256]{1,0:T(8,128)S(1)} custom-call(f32[1024,256]{1,0:T(8,128)S(1)} %get-tuple-element.56.refs_0_, bf16[2048,256]{1,0:T(8,128)(2,1)S(1)} %get-tuple-element.37.refs_0_.refs_1_.s_ref, bf16[512,512]{1,0:T(8,128)(2,1)S(1)} %collective-permute-done.8.refs_2_.refs_0_), custom_call_target="tpu_custom_call", output_to_operand_aliasing={{}: (0, {})} | custom-call | flops 536870912 | bytes 4194304 | tf_op jit(solution)/shard_map/pallas_call | solution.py:191
  55.1 1.4 %shard_map.45 = (bf16[256,256]{1,0:T(8,128)(2,1)S(1)}, bf16[256,256]{1,0:T(8,128)(2,1)S(1)}, bf16[256,256]{1,0:T(8,128)(2,1)S(1)}, bf16[256,256]{1,0:T(8,128)(2,1)S(1)}, f32[256,256]{1,0:T(8,128)S(1)}) custom-call(f32[1024,256]{1,0:T(8,128)S(1)} %get-tuple-element.52.start_ref, bf16[1024,256]{1,0:T(8,128)(2,1)S(1)} %collective-permute-done.7.handed_ref, ...), custom_call_target="tpu_custom_call" | custom-call | flops 1074790400 | bytes 4194304 | tf_op jit(solution)/shard_map/pallas_call | solution.py:225
  57.5 3.7 %collective-permute-start.12 = (bf16[256,256]{1,0:T(8,128)(2,1)S(1)}, bf16[256,256]{1,0:T(8,128)(2,1)S(1)}, u32[]{:S(2)}, u32[]{:S(2)}) collective-permute-start(bf16[256,256]{1,0:T(8,128)(2,1)S(1)} %get-tuple-element.61), channel_id=1, source_target_pairs={{0,6},{1,7},{2,4},{3,5},{4,2},{5,3},{6,0},{7,1},{8,10},{9,11},{10,... | collective-permute-start | bytes 393224 | tf_op jit(solution)/shard_map/ppermute | solution.py:29
  61.9 2.0 %collective-permute-start.14 = (bf16[256,256]{1,0:T(8,128)(2,1)S(1)}, bf16[256,256]{1,0:T(8,128)(2,1)S(1)}, u32[]{:S(2)}, u32[]{:S(2)}) collective-permute-start(bf16[256,256]{1,0:T(8,128)(2,1)S(1)} %get-tuple-element.63), channel_id=1, source_target_pairs={{0,7},{1,4},{2,5},{3,6},{4,3},{5,0},{6,1},{7,2},{8,11},{9,8},{10,9... | collective-permute-start | bytes 393224 | tf_op jit(solution)/shard_map/ppermute | solution.py:29
  65.4 3.0 %collective-permute-start.17 = (bf16[256,256]{1,0:T(8,128)(2,1)S(1)}, bf16[256,256]{1,0:T(8,128)(2,1)S(1)}, u32[]{:S(2)}, u32[]{:S(2)}) collective-permute-start(bf16[256,256]{1,0:T(8,128)(2,1)S(1)} %get-tuple-element.66), channel_id=1, source_target_pairs={{0,3},{1,0},{2,1},{3,2},{4,7},{5,4},{6,5},{7,6},{8,15},{9,12},{10,... | collective-permute-start | bytes 393224 | tf_op jit(solution)/shard_map/ppermute | solution.py:29
  68.3 1.5 %collective-permute-done.13.refs_3_ = bf16[256,256]{1,0:T(8,128)(2,1)S(1)} collective-permute-done((bf16[256,256]{1,0:T(8,128)(2,1)S(1)}, bf16[256,256]{1,0:T(8,128)(2,1)S(1)}, u32[]{:S(2)}, u32[]{:S(2)}) %collective-permute-start.13) | collective-permute-done | bytes 131104 | tf_op jit(solution)/shard_map/ppermute | solution.py:29
  69.8 1.7 %collective-permute-done.15.refs_5_ = bf16[256,256]{1,0:T(8,128)(2,1)S(1)} collective-permute-done((bf16[256,256]{1,0:T(8,128)(2,1)S(1)}, bf16[256,256]{1,0:T(8,128)(2,1)S(1)}, u32[]{:S(2)}, u32[]{:S(2)}) %collective-permute-start.15) | collective-permute-done | bytes 131104 | tf_op jit(solution)/shard_map/ppermute | solution.py:29
  71.5 1.8 %collective-permute-done.16.refs_6_ = bf16[256,256]{1,0:T(8,128)(2,1)S(1)} collective-permute-done((bf16[256,256]{1,0:T(8,128)(2,1)S(1)}, bf16[256,256]{1,0:T(8,128)(2,1)S(1)}, u32[]{:S(2)}, u32[]{:S(2)}) %collective-permute-start.16) | collective-permute-done | bytes 131104 | tf_op jit(solution)/shard_map/ppermute | solution.py:29
  (27 shorter events, 5.5 us)
Async XLA Ops:
  1.8 9.9 %collective-permute-start.1 = (bf16[512,512]{1,0:T(8,128)(2,1)S(1)}, bf16[512,512]{1,0:T(8,128)(2,1)S(1)}, u32[]{:S(2)}, u32[]{:S(2)}) collective-permute-start(bf16[512,512]{1,0:T(8,128)(2,1)S(1)} %pack_data.1.refs_2_), channel_id=1, source_target_pairs={{0,16},{1,17},{2,18},{3,19},{4,20},{5,21},{6,22},{7,23},{8,56},{9,... | collective-permute-start | bytes 1572872 | tf_op jit(solution)/shard_map/ppermute | solution.py:29
  5.1 1.6 %copy-start = (f32[2048,256]{1,0:T(8,128)S(1)}, f32[2048,256]{1,0:T(8,128)}, u32[]{:S(2)}) copy-start(f32[2048,256]{1,0:T(8,128)} %s_hbm.1) | copy-start | bytes 6291460
  8.7 18.7 %collective-permute-start = (bf16[2048,256]{1,0:T(8,128)(2,1)S(1)}, bf16[2048,256]{1,0:T(8,128)(2,1)S(1)}, u32[]{:S(2)}, u32[]{:S(2)}) collective-permute-start(bf16[2048,256]{1,0:T(8,128)(2,1)S(1)} %get-tuple-element.37.refs_0_.refs_1_.s_ref), channel_id=1, source_target_pairs={{0,8},{1,9},{2,10},{3,11},{4,12},{5,13},{6,14},{7,15},{8,0},{9,1},... | collective-permute-start | bytes 3145736 | tf_op jit(solution)/shard_map/ppermute | solution.py:29
  8.8 14.5 %collective-permute-start.2 = (bf16[512,512]{1,0:T(8,128)(2,1)S(1)}, bf16[512,512]{1,0:T(8,128)(2,1)S(1)}, u32[]{:S(2)}, u32[]{:S(2)}) collective-permute-start(bf16[512,512]{1,0:T(8,128)(2,1)S(1)} %pack_data.1.refs_2_), channel_id=1, source_target_pairs={{0,68},{1,69},{2,70},{3,71},{4,64},{5,65},{6,66},{7,67},{8,76},{9,... | collective-permute-start | bytes 1572872 | tf_op jit(solution)/shard_map/ppermute | solution.py:29
  11.7 13.2 %collective-permute-start.4 = (bf16[512,512]{1,0:T(8,128)(2,1)S(1)}, bf16[512,512]{1,0:T(8,128)(2,1)S(1)}, u32[]{:S(2)}, u32[]{:S(2)}) collective-permute-start(bf16[512,512]{1,0:T(8,128)(2,1)S(1)} %collective-permute-done.1.refs_3_), channel_id=1, source_target_pairs={{0,16},{1,17},{2,18},{3,19},{4,20},{5,21},{6,22},{7,23},{8,56},{9,... | collective-permute-start | bytes 1572872 | tf_op jit(solution)/shard_map/ppermute | solution.py:29
  14.7 20.8 %collective-permute-start.3 = (bf16[512,512]{1,0:T(8,128)(2,1)S(1)}, bf16[512,512]{1,0:T(8,128)(2,1)S(1)}, u32[]{:S(2)}, u32[]{:S(2)}) collective-permute-start(bf16[512,512]{1,0:T(8,128)(2,1)S(1)} %pack_data.1.refs_2_), channel_id=1, source_target_pairs={{0,48},{1,49},{2,50},{3,51},{4,52},{5,53},{6,54},{7,55},{8,24},{9,... | collective-permute-start | bytes 1572872 | tf_op jit(solution)/shard_map/ppermute | solution.py:29
  23.3 17.6 %collective-permute-start.5 = (bf16[512,512]{1,0:T(8,128)(2,1)S(1)}, bf16[512,512]{1,0:T(8,128)(2,1)S(1)}, u32[]{:S(2)}, u32[]{:S(2)}) collective-permute-start(bf16[512,512]{1,0:T(8,128)(2,1)S(1)} %collective-permute-done.2.refs_6_), channel_id=1, source_target_pairs={{0,16},{1,17},{2,18},{3,19},{4,20},{5,21},{6,22},{7,23},{8,56},{9,... | collective-permute-start | bytes 1572872 | tf_op jit(solution)/shard_map/ppermute | solution.py:29
  24.8 19.2 %collective-permute-start.6 = (bf16[512,512]{1,0:T(8,128)(2,1)S(1)}, bf16[512,512]{1,0:T(8,128)(2,1)S(1)}, u32[]{:S(2)}, u32[]{:S(2)}) collective-permute-start(bf16[512,512]{1,0:T(8,128)(2,1)S(1)} %collective-permute-done.2.refs_6_), channel_id=1, source_target_pairs={{0,48},{1,49},{2,50},{3,51},{4,52},{5,53},{6,54},{7,55},{8,24},{9,... | collective-permute-start | bytes 1572872 | tf_op jit(solution)/shard_map/ppermute | solution.py:29
  24.8 25.9 %collective-permute-start.8 = (bf16[512,512]{1,0:T(8,128)(2,1)S(1)}, bf16[512,512]{1,0:T(8,128)(2,1)S(1)}, u32[]{:S(2)}, u32[]{:S(2)}) collective-permute-start(bf16[512,512]{1,0:T(8,128)(2,1)S(1)} %collective-permute-done.4.refs_7_), channel_id=1, source_target_pairs={{0,68},{1,69},{2,70},{3,71},{4,64},{5,65},{6,66},{7,67},{8,76},{9,... | collective-permute-start | bytes 1572872 | tf_op jit(solution)/shard_map/ppermute | solution.py:29
  45.8 8.6 %collective-permute-start.10 = (bf16[1024,256]{1,0:T(8,128)(2,1)S(1)}, bf16[1024,256]{1,0:T(8,128)(2,1)S(1)}, u32[]{:S(2)}, u32[]{:S(2)}) collective-permute-start(bf16[1024,256]{1,0:T(8,128)(2,1)S(1)} %get-tuple-element.57), channel_id=1, source_target_pairs={{0,8},{1,9},{2,10},{3,11},{4,12},{5,13},{6,14},{7,15},{8,0},{9,1},... | collective-permute-start | bytes 1572872 | tf_op jit(solution)/shard_map/ppermute | solution.py:29
  50.7 3.7 %collective-permute-start.9 = (bf16[512,512]{1,0:T(8,128)(2,1)S(1)}, bf16[512,512]{1,0:T(8,128)(2,1)S(1)}, u32[]{:S(2)}, u32[]{:S(2)}) collective-permute-start(bf16[512,512]{1,0:T(8,128)(2,1)S(1)} %collective-permute-done.8.refs_2_.refs_0_), channel_id=1, source_target_pairs={{0,8},{1,9},{2,10},{3,11},{4,12},{5,13},{6,14},{7,15},{8,0},{9,1},... | collective-permute-start | bytes 1572872 | tf_op jit(solution)/shard_map/ppermute | solution.py:29
  52.6 2.6 %collective-permute-start.7 = (bf16[1024,256]{1,0:T(8,128)(2,1)S(1)}, bf16[1024,256]{1,0:T(8,128)(2,1)S(1)}, u32[]{:S(2)}, u32[]{:S(2)}) collective-permute-start(bf16[1024,256]{1,0:T(8,128)(2,1)S(1)} %get-tuple-element.53), channel_id=1, source_target_pairs={{0,8},{1,9},{2,10},{3,11},{4,12},{5,13},{6,14},{7,15},{8,0},{9,1},... | collective-permute-start | bytes 1572872 | tf_op jit(solution)/shard_map/ppermute | solution.py:29
  56.6 8.2 %collective-permute-start.11 = (bf16[256,256]{1,0:T(8,128)(2,1)S(1)}, bf16[256,256]{1,0:T(8,128)(2,1)S(1)}, u32[]{:S(2)}, u32[]{:S(2)}) collective-permute-start(bf16[256,256]{1,0:T(8,128)(2,1)S(1)} %get-tuple-element.60), channel_id=1, source_target_pairs={{0,4},{1,5},{2,6},{3,7},{4,0},{5,1},{6,2},{7,3},{8,12},{9,13},{10,... | collective-permute-start | bytes 393224 | tf_op jit(solution)/shard_map/ppermute | solution.py:29
  57.5 7.9 %collective-permute-start.12 = (bf16[256,256]{1,0:T(8,128)(2,1)S(1)}, bf16[256,256]{1,0:T(8,128)(2,1)S(1)}, u32[]{:S(2)}, u32[]{:S(2)}) collective-permute-start(bf16[256,256]{1,0:T(8,128)(2,1)S(1)} %get-tuple-element.61), channel_id=1, source_target_pairs={{0,6},{1,7},{2,4},{3,5},{4,2},{5,3},{6,0},{7,1},{8,10},{9,11},{10,... | collective-permute-start | bytes 393224 | tf_op jit(solution)/shard_map/ppermute | solution.py:29
  61.2 8.6 %collective-permute-start.13 = (bf16[256,256]{1,0:T(8,128)(2,1)S(1)}, bf16[256,256]{1,0:T(8,128)(2,1)S(1)}, u32[]{:S(2)}, u32[]{:S(2)}) collective-permute-start(bf16[256,256]{1,0:T(8,128)(2,1)S(1)} %get-tuple-element.62), channel_id=1, source_target_pairs={{0,5},{1,6},{2,7},{3,4},{4,1},{5,2},{6,3},{7,0},{8,9},{9,10},{10,1... | collective-permute-start | bytes 393224 | tf_op jit(solution)/shard_map/ppermute | solution.py:29
  61.9 7.9 %collective-permute-start.14 = (bf16[256,256]{1,0:T(8,128)(2,1)S(1)}, bf16[256,256]{1,0:T(8,128)(2,1)S(1)}, u32[]{:S(2)}, u32[]{:S(2)}) collective-permute-start(bf16[256,256]{1,0:T(8,128)(2,1)S(1)} %get-tuple-element.63), channel_id=1, source_target_pairs={{0,7},{1,4},{2,5},{3,6},{4,3},{5,0},{6,1},{7,2},{8,11},{9,8},{10,9... | collective-permute-start | bytes 393224 | tf_op jit(solution)/shard_map/ppermute | solution.py:29
  63.9 7.7 %collective-permute-start.15 = (bf16[256,256]{1,0:T(8,128)(2,1)S(1)}, bf16[256,256]{1,0:T(8,128)(2,1)S(1)}, u32[]{:S(2)}, u32[]{:S(2)}) collective-permute-start(bf16[256,256]{1,0:T(8,128)(2,1)S(1)} %get-tuple-element.64), channel_id=1, source_target_pairs={{0,2},{1,3},{2,0},{3,1},{4,6},{5,7},{6,4},{7,5},{8,14},{9,15},{10,... | collective-permute-start | bytes 393224 | tf_op jit(solution)/shard_map/ppermute | solution.py:29
  64.8 8.6 %collective-permute-start.16 = (bf16[256,256]{1,0:T(8,128)(2,1)S(1)}, bf16[256,256]{1,0:T(8,128)(2,1)S(1)}, u32[]{:S(2)}, u32[]{:S(2)}) collective-permute-start(bf16[256,256]{1,0:T(8,128)(2,1)S(1)} %get-tuple-element.65), channel_id=1, source_target_pairs={{0,1},{1,2},{2,3},{3,0},{4,5},{5,6},{6,7},{7,4},{8,13},{9,14},{10,... | collective-permute-start | bytes 393224 | tf_op jit(solution)/shard_map/ppermute | solution.py:29
  65.4 8.1 %collective-permute-start.17 = (bf16[256,256]{1,0:T(8,128)(2,1)S(1)}, bf16[256,256]{1,0:T(8,128)(2,1)S(1)}, u32[]{:S(2)}, u32[]{:S(2)}) collective-permute-start(bf16[256,256]{1,0:T(8,128)(2,1)S(1)} %get-tuple-element.66), channel_id=1, source_target_pairs={{0,3},{1,0},{2,1},{3,2},{4,7},{5,4},{6,5},{7,6},{8,15},{9,12},{10,... | collective-permute-start | bytes 393224 | tf_op jit(solution)/shard_map/ppermute | solution.py:29

commit v2 on v1

--- a/solution.py
+++ b/solution.py
@@ -131,20 +131,27 @@
     )(state)
 
 
-def tile_sum(state, chunks, start, members, width=256):
-    total = start
-    for chunk in chunks:
-        for c in range(0, chunk.shape[0], width):
-            correl = lax.dot_general(
-                state,
-                chunk[c : c + width, 0:members],
-                (((1,), (1,)), ((), ())),
-                preferred_element_type=jnp.float32,
-            ) * (1.0 / (members - 1))
-            localized = (correl * correl * correl).astype(jnp.bfloat16)
-            part = jnp.dot(localized, chunk[c : c + width, members:], preferred_element_type=jnp.float32)
-            total = part if total is None else total + part
-    return total
+def correlations(state, chunk, members):
+    return lax.dot_general(
+        state, chunk[:, 0:members], (((1,), (1,)), ((), ())), preferred_element_type=jnp.float32
+    ) * (1.0 / (members - 1))
+
+
+def tile_sums(states, starts, chunks, members):
+    steps = [(tile, chunk) for tile in range(len(states)) for chunk in range(len(chunks))]
+    totals = list(starts)
+    ahead = None
+    for n, (tile, chunk) in enumerate(steps):
+        correl = correlations(states[tile](), chunks[chunk][...], members) if ahead is None else ahead
+        ahead = None
+        if n + 1 < len(steps):
+            ahead = correlations(states[steps[n + 1][0]](), chunks[steps[n + 1][1]][...], members)
+        localized = (correl * correl * correl).astype(jnp.bfloat16)
+        part = jnp.dot(localized, chunks[chunk][:, members:], preferred_element_type=jnp.float32)
+        start = totals[tile]() if chunk == 0 and totals[tile] is not None else totals[tile]
+        totals[tile] = part if start is None else start + part
+        if chunk == len(chunks) - 1:
+            yield totals[tile]
 
 
 def half_start(first, mine, half):
@@ -153,7 +160,7 @@
     return lax.rem(lo + core + (1 if first == mine else 0), 2) * half
 
 
-def add_chunks(parts, chunks, sent_kinds=(), tile=1024):
+def add_chunks(parts, chunks, sent_kinds=()):
     members = chunks[0].shape[1] // 2
     half = parts[0][1].shape[0] // 2
     kinds = [jnp.bfloat16 if k in sent_kinds else jnp.float32 for k in range(len(parts))]
@@ -172,21 +179,13 @@
 
     def body(*refs):
         x_refs, o_refs = refs[count : len(operands)], refs[len(operands) :]
-        for (start_at, state_at, which), o_ref in zip(places, o_refs):
-            base = half_start(*which, half)
-
-            def step(i, _):
-                there = pl.ds(pl.multiple_of(i * tile, tile), tile)
-                part = pl.ds(pl.multiple_of(base + i * tile, tile), tile)
-                start = None if start_at is None else refs[start_at][there, :]
-                total = tile_sum(refs[state_at][part, :], x_refs, start, members)
-                o_ref[there, :] = total.astype(o_ref.dtype)
-                return 0
-
-            if tile == half:
-                step(0, 0)
-            else:
-                lax.fori_loop(0, half // tile, step, 0)
+        states, starts = [], []
+        for start_at, state_at, which in places:
+            base = pl.multiple_of(half_start(*which, half), half)
+            states.append(lambda at=state_at, base=base: refs[at][pl.ds(base, half), :])
+            starts.append(None if start_at is None else lambda at=start_at: refs[at][...])
+        for total, o_ref in zip(tile_sums(states, starts, x_refs, members), o_refs):
+            o_ref[...] = total.astype(o_ref.dtype)
 
     return pl.pallas_call(
         body,
@@ -210,7 +209,8 @@
         rows = [pl.multiple_of(lax.rem(z + k, 4) * own, own) for k in steps]
         totals = [start_ref[pl.ds(r, own), :] + handed_ref[pl.ds(r, own), :].astype(jnp.float32) for r in rows]
         state_rows = jnp.concatenate([s_ref[pl.ds(base + r, own), :] for r in rows], axis=0)
-        total = tile_sum(state_rows, x_refs, jnp.concatenate(totals, axis=0), members)
+        start = jnp.concatenate(totals, axis=0)
+        (total,) = tile_sums([lambda: state_rows], [lambda: start], x_refs, members)
         blocks = [total[j * own : (j + 1) * own, :] for j in range(len(steps))]
         if kept is not None:
             upper = jnp.full(blocks[-1].shape, lax.rem(lax.axis_index("state"), 2)) == 1
@@ -278,8 +278,8 @@
     y2s = sent(y2, other_core)
     (fs,) = add_chunks([(fs, s, True, True)], [y2])
     blocks = {}
-    blocks[0, 2], blocks[0, 1] = last_chunks(fs, fh, s, [y2s], own, True, (2, 1))
-    blocks[0, 3], kept = last_chunks(fs, fh, s, [y2s], own, True, (3, 0))
+    blocks[0, 1], blocks[0, 3] = last_chunks(fs, fh, s, [y2s], own, True, (1, 3))
+    blocks[0, 2], kept = last_chunks(fs, fh, s, [y2s], own, True, (2, 0))
     second = last_chunks(ns, nh, s, [y2, y2s], own, False, (2, 1, 3, 0), kept)
     blocks[1, 2], blocks[1, 1], blocks[1, 3], across, mine = second
     arrived = [mine, sent(across, lambda x, y, z, core: (x, y ^ 1, z, core))]

time: 75.6 us -> 72.6 us (0.960)
  the two profiles are of different devices: /device:TPU:1 before, /device:TPU:0 now
where the time goes in v2:
time: 72.6 us; the launch traced here: 72.5 us
  starting transfers between devices  28.5 us (39%)
  Pallas kernels  25.7 us (35%)
  waiting for transfers between devices  16.5 us (23%)
  local copies, waits for them, and re-layouts  1.59 us (2%)
    ppermute x18, starting transfers between devices, sent(): lax.ppermute(value, AXES, [(i, index(*to(*place(i)))) for i in range(128)])  28.5 us
    pallas_call x7, Pallas kernels, add_chunks(): pl.pallas_call(body, out_shape=[jax.ShapeDtypeStruct((half, members), kin...  18.5 us
    ppermute x18, waiting for transfers between devices, sent(): lax.ppermute(value, AXES, [(i, index(*to(*place(i)))) for i in range(128)])  16.5 us
    pallas_call x3, Pallas kernels, last_chunks(): pl.pallas_call(body, out_shape=[jax.ShapeDtypeStruct((own, members), kind...  2.55 us
    pallas_call x1, Pallas kernels, prepare_state(): pl.pallas_call(body, out_shape=(jax.ShapeDtypeStruct((rows, members), jnp...  2.01 us
    pallas_call x1, Pallas kernels, pack_data(): pl.pallas_call(body, out_shape=jax.ShapeDtypeStruct((rows, 2 * members),...  1.76 us
    unnamed x2, local copies, waits for them, and re-layouts  1.59 us
  transfers between devices with their start and end apart: 18, of which 7 were waited for; matrix products, arithmetic and copies ran while one was open for 0% of the time, Pallas kernels for 30%

profile of v2, /device:TPU:0, one launch (start us, length us, event | category | flops | bytes accessed | tf_op | source)
XLA Modules:
  0.0 72.5 jit_solution(10260138809570433356)
XLA Ops:
  0.0 1.8 %pack_data.1.refs_2_ = bf16[512,512]{1,0:T(8,128)(2,1)S(1)} custom-call(f32[512,256]{1,0:T(8,128)} %p_hbm.1, bf16[512,256]{1,0:T(8,128)(2,1)} %i_hbm.1), custom_call_target="tpu_custom_call" | custom-call | flops 1048576 | bytes 1048576 | tf_op jit(solution)/shard_map/pack_data/pallas_call | solution.py:79
  1.8 1.7 %collective-permute-start.1 = (bf16[512,512]{1,0:T(8,128)(2,1)S(1)}, bf16[512,512]{1,0:T(8,128)(2,1)S(1)}, u32[]{:S(2)}, u32[]{:S(2)}) collective-permute-start(bf16[512,512]{1,0:T(8,128)(2,1)S(1)} %pack_data.1.refs_2_), channel_id=1, source_target_pairs={{0,16},{1,17},{2,18},{3,19},{4,20},{5,21},{6,22},{7,23},{8,56},{9,... | collective-permute-start | bytes 1572872 | tf_op jit(solution)/shard_map/ppermute | solution.py:29
  3.4 1.6 %copy-done = f32[2048,256]{1,0:T(8,128)S(1)} copy-done((f32[2048,256]{1,0:T(8,128)S(1)}, f32[2048,256]{1,0:T(8,128)}, u32[]{:S(2)}) %copy-start) | copy-done | bytes 2097176
  5.0 2.0 %prepare_state.1 = (bf16[2048,256]{1,0:T(8,128)(2,1)S(1)}, f32[256,256]{1,0:T(8,128)S(1)}) custom-call(f32[2048,256]{1,0:T(8,128)S(1)} %copy-done), custom_call_target="tpu_custom_call" | custom-call | flops 16777216 | bytes 4194304 | tf_op jit(solution)/shard_map/prepare_state/pallas_call | solution.py:119
  8.0 3.0 %collective-permute-start.2 = (bf16[512,512]{1,0:T(8,128)(2,1)S(1)}, bf16[512,512]{1,0:T(8,128)(2,1)S(1)}, u32[]{:S(2)}, u32[]{:S(2)}) collective-permute-start(bf16[512,512]{1,0:T(8,128)(2,1)S(1)} %pack_data.1.refs_2_), channel_id=1, source_target_pairs={{0,68},{1,69},{2,70},{3,71},{4,64},{5,65},{6,66},{7,67},{8,76},{9,... | collective-permute-start | bytes 1572872 | tf_op jit(solution)/shard_map/ppermute | solution.py:29
  11.0 1.3 %collective-permute-done.1.refs_3_ = bf16[512,512]{1,0:T(8,128)(2,1)S(1)} collective-permute-done((bf16[512,512]{1,0:T(8,128)(2,1)S(1)}, bf16[512,512]{1,0:T(8,128)(2,1)S(1)}, u32[]{:S(2)}, u32[]{:S(2)}) %collective-permute-start.1) | collective-permute-done | bytes 524320 | tf_op jit(solution)/shard_map/ppermute | solution.py:29
  12.6 2.8 %collective-permute-start.3 = (bf16[512,512]{1,0:T(8,128)(2,1)S(1)}, bf16[512,512]{1,0:T(8,128)(2,1)S(1)}, u32[]{:S(2)}, u32[]{:S(2)}) collective-permute-start(bf16[512,512]{1,0:T(8,128)(2,1)S(1)} %pack_data.1.refs_2_), channel_id=1, source_target_pairs={{0,48},{1,49},{2,50},{3,51},{4,52},{5,53},{6,54},{7,55},{8,24},{9,... | collective-permute-start | bytes 1572872 | tf_op jit(solution)/shard_map/ppermute | solution.py:29
  15.5 7.7 %collective-permute-done.2.refs_6_ = bf16[512,512]{1,0:T(8,128)(2,1)S(1)} collective-permute-done((bf16[512,512]{1,0:T(8,128)(2,1)S(1)}, bf16[512,512]{1,0:T(8,128)(2,1)S(1)}, u32[]{:S(2)}, u32[]{:S(2)}) %collective-permute-start.2) | collective-permute-done | bytes 524320 | tf_op jit(solution)/shard_map/ppermute | solution.py:29
  24.2 2.2 %collective-permute-start.6 = (bf16[512,512]{1,0:T(8,128)(2,1)S(1)}, bf16[512,512]{1,0:T(8,128)(2,1)S(1)}, u32[]{:S(2)}, u32[]{:S(2)}) collective-permute-start(bf16[512,512]{1,0:T(8,128)(2,1)S(1)} %collective-permute-done.2.refs_6_), channel_id=1, source_target_pairs={{0,48},{1,49},{2,50},{3,51},{4,52},{5,53},{6,54},{7,55},{8,24},{9,... | collective-permute-start | bytes 1572872 | tf_op jit(solution)/shard_map/ppermute | solution.py:29
  27.6 3.2 %collective-permute-start.8 = (bf16[512,512]{1,0:T(8,128)(2,1)S(1)}, bf16[512,512]{1,0:T(8,128)(2,1)S(1)}, u32[]{:S(2)}, u32[]{:S(2)}) collective-permute-start(bf16[512,512]{1,0:T(8,128)(2,1)S(1)} %collective-permute-done.4.refs_7_), channel_id=1, source_target_pairs={{0,68},{1,69},{2,70},{3,71},{4,64},{5,65},{6,66},{7,67},{8,76},{9,... | collective-permute-start | bytes 1572872 | tf_op jit(solution)/shard_map/ppermute | solution.py:29
  30.9 4.6 %shard_map.37 = (f32[1024,256]{1,0:T(8,128)S(1)}, f32[1024,256]{1,0:T(8,128)S(1)}, f32[1024,256]{1,0:T(8,128)S(1)}, f32[1024,256]{1,0:T(8,128)S(1)}) custom-call(bf16[2048,256]{1,0:T(8,128)(2,1)S(1)} %get-tuple-element.37.refs_0_.refs_1_.s_ref, bf16[2048,256]{1,0:T(8,128)(2,1)S(1)} %collective-permute-done.refs_1_.refs_3_, ...), custom_call_target="tpu_custom_call" | custom-call | flops 4294967296 | bytes 4194304 | tf_op jit(solution)/shard_map/pallas_call | solution.py:190
  35.4 2.6 %shard_map.38 = (f32[1024,256]{1,0:T(8,128)S(1)}, f32[1024,256]{1,0:T(8,128)S(1)}, f32[1024,256]{1,0:T(8,128)S(1)}, f32[1024,256]{1,0:T(8,128)S(1)}) custom-call(f32[1024,256]{1,0:T(8,128)S(1)} %get-tuple-element.38.refs_0_, ...), custom_call_target="tpu_custom_call", output_to_operand_aliasing={{0}: (0, {}), {1}: (2, {}), {2}: (4, {}), {3}: (5, {})} | custom-call | flops 2147483648 | bytes 4194304 | tf_op jit(solution)/shard_map/pallas_call | solution.py:190
  38.1 5.0 %shard_map.39 = (f32[1024,256]{1,0:T(8,128)S(1)}, f32[1024,256]{1,0:T(8,128)S(1)}, f32[1024,256]{1,0:T(8,128)S(1)}, f32[1024,256]{1,0:T(8,128)S(1)}) custom-call(f32[1024,256]{1,0:T(8,128)S(1)} %get-tuple-element.42.refs_0_, ...), custom_call_target="tpu_custom_call", output_to_operand_aliasing={{0}: (0, {}), {1}: (2, {}), {2}: (4, {}), {3}: (5, {})} | custom-call | flops 4294967296 | bytes 4194304 | tf_op jit(solution)/shard_map/pallas_call | solution.py:190
  43.1 2.8 %shard_map.40 = (f32[1024,256]{1,0:T(8,128)S(1)}, f32[1024,256]{1,0:T(8,128)S(1)}, f32[1024,256]{1,0:T(8,128)S(1)}, f32[1024,256]{1,0:T(8,128)S(1)}) custom-call(f32[1024,256]{1,0:T(8,128)S(1)} %get-tuple-element.46.refs_0_, ...), custom_call_target="tpu_custom_call", output_to_operand_aliasing={{0}: (0, {}), {1}: (2, {}), {2}: (4, {}), {3}: (5, {})} | custom-call | flops 2147483648 | bytes 4194304 | tf_op jit(solution)/shard_map/pallas_call | solution.py:190
  45.9 1.3 %shard_map.42 = (f32[1024,256]{1,0:T(8,128)S(1)}, bf16[1024,256]{1,0:T(8,128)(2,1)S(1)}) custom-call(f32[1024,256]{1,0:T(8,128)S(1)} %get-tuple-element.54.refs_0_, bf16[2048,256]{1,0:T(8,128)(2,1)S(1)} %get-tuple-element.37.refs_0_.refs_1_.s_ref, f32[1024,256]{1,0:T(8,128)S(1)} %get-tuple-element.55.refs_2_, ...), custom_call_target="tpu_custom_call", output_to_operand_aliasing={{0}: (0, {})} | custom-call | flops 1073741824 | bytes 4194304 | tf_op jit(solution)/shard_map/pallas_call | solution.py:190
  47.8 1.3 %shard_map.41 = (f32[1024,256]{1,0:T(8,128)S(1)}, bf16[1024,256]{1,0:T(8,128)(2,1)S(1)}) custom-call(f32[1024,256]{1,0:T(8,128)S(1)} %get-tuple-element.50.refs_0_, bf16[2048,256]{1,0:T(8,128)(2,1)S(1)} %get-tuple-element.37.refs_0_.refs_1_.s_ref, f32[1024,256]{1,0:T(8,128)S(1)} %get-tuple-element.51.refs_2_, ...), custom_call_target="tpu_custom_call", output_to_operand_aliasing={{0}: (0, {})} | custom-call | flops 1073741824 | bytes 4194304 | tf_op jit(solution)/shard_map/pallas_call | solution.py:190
  51.2 1.4 %shard_map.45 = (bf16[256,256]{1,0:T(8,128)(2,1)S(1)}, bf16[256,256]{1,0:T(8,128)(2,1)S(1)}, bf16[256,256]{1,0:T(8,128)(2,1)S(1)}, bf16[256,256]{1,0:T(8,128)(2,1)S(1)}, f32[256,256]{1,0:T(8,128)S(1)}) custom-call(f32[1024,256]{1,0:T(8,128)S(1)} %get-tuple-element.52.start_ref, bf16[1024,256]{1,0:T(8,128)(2,1)S(1)} %collective-permute-done.7.handed_ref, ...), custom_call_target="tpu_custom_call" | custom-call | flops 1074790400 | bytes 4194304 | tf_op jit(solution)/shard_map/pallas_call | solution.py:225
  53.7 3.0 %collective-permute-start.12 = (bf16[256,256]{1,0:T(8,128)(2,1)S(1)}, bf16[256,256]{1,0:T(8,128)(2,1)S(1)}, u32[]{:S(2)}, u32[]{:S(2)}) collective-permute-start(bf16[256,256]{1,0:T(8,128)(2,1)S(1)} %get-tuple-element.61), channel_id=1, source_target_pairs={{0,5},{1,6},{2,7},{3,4},{4,1},{5,2},{6,3},{7,0},{8,9},{9,10},{10,1... | collective-permute-start | bytes 393224 | tf_op jit(solution)/shard_map/ppermute | solution.py:29
  56.7 2.2 %collective-permute-start.13 = (bf16[256,256]{1,0:T(8,128)(2,1)S(1)}, bf16[256,256]{1,0:T(8,128)(2,1)S(1)}, u32[]{:S(2)}, u32[]{:S(2)}) collective-permute-start(bf16[256,256]{1,0:T(8,128)(2,1)S(1)} %get-tuple-element.62), channel_id=1, source_target_pairs={{0,7},{1,4},{2,5},{3,6},{4,3},{5,0},{6,1},{7,2},{8,11},{9,8},{10,9... | collective-permute-start | bytes 393224 | tf_op jit(solution)/shard_map/ppermute | solution.py:29
  58.9 2.7 %collective-permute-start.14 = (bf16[256,256]{1,0:T(8,128)(2,1)S(1)}, bf16[256,256]{1,0:T(8,128)(2,1)S(1)}, u32[]{:S(2)}, u32[]{:S(2)}) collective-permute-start(bf16[256,256]{1,0:T(8,128)(2,1)S(1)} %get-tuple-element.63), channel_id=1, source_target_pairs={{0,6},{1,7},{2,4},{3,5},{4,2},{5,3},{6,0},{7,1},{8,10},{9,11},{10,... | collective-permute-start | bytes 393224 | tf_op jit(solution)/shard_map/ppermute | solution.py:29
  63.2 2.5 %collective-permute-start.17 = (bf16[256,256]{1,0:T(8,128)(2,1)S(1)}, bf16[256,256]{1,0:T(8,128)(2,1)S(1)}, u32[]{:S(2)}, u32[]{:S(2)}) collective-permute-start(bf16[256,256]{1,0:T(8,128)(2,1)S(1)} %get-tuple-element.66), channel_id=1, source_target_pairs={{0,3},{1,0},{2,1},{3,2},{4,7},{5,4},{6,5},{7,6},{8,15},{9,12},{10,... | collective-permute-start | bytes 393224 | tf_op jit(solution)/shard_map/ppermute | solution.py:29
  65.7 2.8 %collective-permute-done.14.refs_4_ = bf16[256,256]{1,0:T(8,128)(2,1)S(1)} collective-permute-done((bf16[256,256]{1,0:T(8,128)(2,1)S(1)}, bf16[256,256]{1,0:T(8,128)(2,1)S(1)}, u32[]{:S(2)}, u32[]{:S(2)}) %collective-permute-start.14) | collective-permute-done | bytes 131104 | tf_op jit(solution)/shard_map/ppermute | solution.py:29
  68.4 1.9 %collective-permute-done.15.refs_5_ = bf16[256,256]{1,0:T(8,128)(2,1)S(1)} collective-permute-done((bf16[256,256]{1,0:T(8,128)(2,1)S(1)}, bf16[256,256]{1,0:T(8,128)(2,1)S(1)}, u32[]{:S(2)}, u32[]{:S(2)}) %collective-permute-start.15) | collective-permute-done | bytes 131104 | tf_op jit(solution)/shard_map/ppermute | solution.py:29
  70.3 1.3 %collective-permute-done.16.refs_6_ = bf16[256,256]{1,0:T(8,128)(2,1)S(1)} collective-permute-done((bf16[256,256]{1,0:T(8,128)(2,1)S(1)}, bf16[256,256]{1,0:T(8,128)(2,1)S(1)}, u32[]{:S(2)}, u32[]{:S(2)}) %collective-permute-start.16) | collective-permute-done | bytes 131104 | tf_op jit(solution)/shard_map/ppermute | solution.py:29
  (27 shorter events, 9.7 us)
Async XLA Ops:
  1.8 10.5 %collective-permute-start.1 = (bf16[512,512]{1,0:T(8,128)(2,1)S(1)}, bf16[512,512]{1,0:T(8,128)(2,1)S(1)}, u32[]{:S(2)}, u32[]{:S(2)}) collective-permute-start(bf16[512,512]{1,0:T(8,128)(2,1)S(1)} %pack_data.1.refs_2_), channel_id=1, source_target_pairs={{0,16},{1,17},{2,18},{3,19},{4,20},{5,21},{6,22},{7,23},{8,56},{9,... | collective-permute-start | bytes 1572872 | tf_op jit(solution)/shard_map/ppermute | solution.py:29
  3.4 1.6 %copy-start = (f32[2048,256]{1,0:T(8,128)S(1)}, f32[2048,256]{1,0:T(8,128)}, u32[]{:S(2)}) copy-start(f32[2048,256]{1,0:T(8,128)} %s_hbm.1) | copy-start | bytes 6291460
  7.0 23.8 %collective-permute-start = (bf16[2048,256]{1,0:T(8,128)(2,1)S(1)}, bf16[2048,256]{1,0:T(8,128)(2,1)S(1)}, u32[]{:S(2)}, u32[]{:S(2)}) collective-permute-start(bf16[2048,256]{1,0:T(8,128)(2,1)S(1)} %get-tuple-element.37.refs_0_.refs_1_.s_ref), channel_id=1, source_target_pairs={{0,8},{1,9},{2,10},{3,11},{4,12},{5,13},{6,14},{7,15},{8,0},{9,1},... | collective-permute-start | bytes 3145736 | tf_op jit(solution)/shard_map/ppermute | solution.py:29
  8.0 15.2 %collective-permute-start.2 = (bf16[512,512]{1,0:T(8,128)(2,1)S(1)}, bf16[512,512]{1,0:T(8,128)(2,1)S(1)}, u32[]{:S(2)}, u32[]{:S(2)}) collective-permute-start(bf16[512,512]{1,0:T(8,128)(2,1)S(1)} %pack_data.1.refs_2_), channel_id=1, source_target_pairs={{0,68},{1,69},{2,70},{3,71},{4,64},{5,65},{6,66},{7,67},{8,76},{9,... | collective-permute-start | bytes 1572872 | tf_op jit(solution)/shard_map/ppermute | solution.py:29
  12.2 15.4 %collective-permute-start.4 = (bf16[512,512]{1,0:T(8,128)(2,1)S(1)}, bf16[512,512]{1,0:T(8,128)(2,1)S(1)}, u32[]{:S(2)}, u32[]{:S(2)}) collective-permute-start(bf16[512,512]{1,0:T(8,128)(2,1)S(1)} %collective-permute-done.1.refs_3_), channel_id=1, source_target_pairs={{0,16},{1,17},{2,18},{3,19},{4,20},{5,21},{6,22},{7,23},{8,56},{9,... | collective-permute-start | bytes 1572872 | tf_op jit(solution)/shard_map/ppermute | solution.py:29
  12.6 25.4 %collective-permute-start.3 = (bf16[512,512]{1,0:T(8,128)(2,1)S(1)}, bf16[512,512]{1,0:T(8,128)(2,1)S(1)}, u32[]{:S(2)}, u32[]{:S(2)}) collective-permute-start(bf16[512,512]{1,0:T(8,128)(2,1)S(1)} %pack_data.1.refs_2_), channel_id=1, source_target_pairs={{0,48},{1,49},{2,50},{3,51},{4,52},{5,53},{6,54},{7,55},{8,24},{9,... | collective-permute-start | bytes 1572872 | tf_op jit(solution)/shard_map/ppermute | solution.py:29
  23.1 19.9 %collective-permute-start.5 = (bf16[512,512]{1,0:T(8,128)(2,1)S(1)}, bf16[512,512]{1,0:T(8,128)(2,1)S(1)}, u32[]{:S(2)}, u32[]{:S(2)}) collective-permute-start(bf16[512,512]{1,0:T(8,128)(2,1)S(1)} %collective-permute-done.2.refs_6_), channel_id=1, source_target_pairs={{0,16},{1,17},{2,18},{3,19},{4,20},{5,21},{6,22},{7,23},{8,56},{9,... | collective-permute-start | bytes 1572872 | tf_op jit(solution)/shard_map/ppermute | solution.py:29
  24.2 21.7 %collective-permute-start.6 = (bf16[512,512]{1,0:T(8,128)(2,1)S(1)}, bf16[512,512]{1,0:T(8,128)(2,1)S(1)}, u32[]{:S(2)}, u32[]{:S(2)}) collective-permute-start(bf16[512,512]{1,0:T(8,128)(2,1)S(1)} %collective-permute-done.2.refs_6_), channel_id=1, source_target_pairs={{0,48},{1,49},{2,50},{3,51},{4,52},{5,53},{6,54},{7,55},{8,24},{9,... | collective-permute-start | bytes 1572872 | tf_op jit(solution)/shard_map/ppermute | solution.py:29
  27.6 19.7 %collective-permute-start.8 = (bf16[512,512]{1,0:T(8,128)(2,1)S(1)}, bf16[512,512]{1,0:T(8,128)(2,1)S(1)}, u32[]{:S(2)}, u32[]{:S(2)}) collective-permute-start(bf16[512,512]{1,0:T(8,128)(2,1)S(1)} %collective-permute-done.4.refs_7_), channel_id=1, source_target_pairs={{0,68},{1,69},{2,70},{3,71},{4,64},{5,65},{6,66},{7,67},{8,76},{9,... | collective-permute-start | bytes 1572872 | tf_op jit(solution)/shard_map/ppermute | solution.py:29
  47.2 3.0 %collective-permute-start.10 = (bf16[1024,256]{1,0:T(8,128)(2,1)S(1)}, bf16[1024,256]{1,0:T(8,128)(2,1)S(1)}, u32[]{:S(2)}, u32[]{:S(2)}) collective-permute-start(bf16[1024,256]{1,0:T(8,128)(2,1)S(1)} %get-tuple-element.57), channel_id=1, source_target_pairs={{0,8},{1,9},{2,10},{3,11},{4,12},{5,13},{6,14},{7,15},{8,0},{9,1},... | collective-permute-start | bytes 1572872 | tf_op jit(solution)/shard_map/ppermute | solution.py:29
  47.3 2.9 %collective-permute-start.9 = (bf16[512,512]{1,0:T(8,128)(2,1)S(1)}, bf16[512,512]{1,0:T(8,128)(2,1)S(1)}, u32[]{:S(2)}, u32[]{:S(2)}) collective-permute-start(bf16[512,512]{1,0:T(8,128)(2,1)S(1)} %collective-permute-done.8.refs_2_.refs_0_), channel_id=1, source_target_pairs={{0,8},{1,9},{2,10},{3,11},{4,12},{5,13},{6,14},{7,15},{8,0},{9,1},... | collective-permute-start | bytes 1572872 | tf_op jit(solution)/shard_map/ppermute | solution.py:29
  49.2 2.0 %collective-permute-start.7 = (bf16[1024,256]{1,0:T(8,128)(2,1)S(1)}, bf16[1024,256]{1,0:T(8,128)(2,1)S(1)}, u32[]{:S(2)}, u32[]{:S(2)}) collective-permute-start(bf16[1024,256]{1,0:T(8,128)(2,1)S(1)} %get-tuple-element.53), channel_id=1, source_target_pairs={{0,8},{1,9},{2,10},{3,11},{4,12},{5,13},{6,14},{7,15},{8,0},{9,1},... | collective-permute-start | bytes 1572872 | tf_op jit(solution)/shard_map/ppermute | solution.py:29
  52.6 9.9 %collective-permute-start.11 = (bf16[256,256]{1,0:T(8,128)(2,1)S(1)}, bf16[256,256]{1,0:T(8,128)(2,1)S(1)}, u32[]{:S(2)}, u32[]{:S(2)}) collective-permute-start(bf16[256,256]{1,0:T(8,128)(2,1)S(1)} %get-tuple-element.60), channel_id=1, source_target_pairs={{0,4},{1,5},{2,6},{3,7},{4,0},{5,1},{6,2},{7,3},{8,12},{9,13},{10,... | collective-permute-start | bytes 393224 | tf_op jit(solution)/shard_map/ppermute | solution.py:29
  53.7 9.5 %collective-permute-start.12 = (bf16[256,256]{1,0:T(8,128)(2,1)S(1)}, bf16[256,256]{1,0:T(8,128)(2,1)S(1)}, u32[]{:S(2)}, u32[]{:S(2)}) collective-permute-start(bf16[256,256]{1,0:T(8,128)(2,1)S(1)} %get-tuple-element.61), channel_id=1, source_target_pairs={{0,5},{1,6},{2,7},{3,4},{4,1},{5,2},{6,3},{7,0},{8,9},{9,10},{10,1... | collective-permute-start | bytes 393224 | tf_op jit(solution)/shard_map/ppermute | solution.py:29
  56.7 9.0 %collective-permute-start.13 = (bf16[256,256]{1,0:T(8,128)(2,1)S(1)}, bf16[256,256]{1,0:T(8,128)(2,1)S(1)}, u32[]{:S(2)}, u32[]{:S(2)}) collective-permute-start(bf16[256,256]{1,0:T(8,128)(2,1)S(1)} %get-tuple-element.62), channel_id=1, source_target_pairs={{0,7},{1,4},{2,5},{3,6},{4,3},{5,0},{6,1},{7,2},{8,11},{9,8},{10,9... | collective-permute-start | bytes 393224 | tf_op jit(solution)/shard_map/ppermute | solution.py:29
  58.9 9.6 %collective-permute-start.14 = (bf16[256,256]{1,0:T(8,128)(2,1)S(1)}, bf16[256,256]{1,0:T(8,128)(2,1)S(1)}, u32[]{:S(2)}, u32[]{:S(2)}) collective-permute-start(bf16[256,256]{1,0:T(8,128)(2,1)S(1)} %get-tuple-element.63), channel_id=1, source_target_pairs={{0,6},{1,7},{2,4},{3,5},{4,2},{5,3},{6,0},{7,1},{8,10},{9,11},{10,... | collective-permute-start | bytes 393224 | tf_op jit(solution)/shard_map/ppermute | solution.py:29
  61.6 8.8 %collective-permute-start.15 = (bf16[256,256]{1,0:T(8,128)(2,1)S(1)}, bf16[256,256]{1,0:T(8,128)(2,1)S(1)}, u32[]{:S(2)}, u32[]{:S(2)}) collective-permute-start(bf16[256,256]{1,0:T(8,128)(2,1)S(1)} %get-tuple-element.64), channel_id=1, source_target_pairs={{0,2},{1,3},{2,0},{3,1},{4,6},{5,7},{6,4},{7,5},{8,14},{9,15},{10,... | collective-permute-start | bytes 393224 | tf_op jit(solution)/shard_map/ppermute | solution.py:29
  62.4 9.2 %collective-permute-start.16 = (bf16[256,256]{1,0:T(8,128)(2,1)S(1)}, bf16[256,256]{1,0:T(8,128)(2,1)S(1)}, u32[]{:S(2)}, u32[]{:S(2)}) collective-permute-start(bf16[256,256]{1,0:T(8,128)(2,1)S(1)} %get-tuple-element.65), channel_id=1, source_target_pairs={{0,1},{1,2},{2,3},{3,0},{4,5},{5,6},{6,7},{7,4},{8,13},{9,14},{10,... | collective-permute-start | bytes 393224 | tf_op jit(solution)/shard_map/ppermute | solution.py:29
  63.2 8.5 %collective-permute-start.17 = (bf16[256,256]{1,0:T(8,128)(2,1)S(1)}, bf16[256,256]{1,0:T(8,128)(2,1)S(1)}, u32[]{:S(2)}, u32[]{:S(2)}) collective-permute-start(bf16[256,256]{1,0:T(8,128)(2,1)S(1)} %get-tuple-element.66), channel_id=1, source_target_pairs={{0,3},{1,0},{2,1},{3,2},{4,7},{5,4},{6,5},{7,6},{8,15},{9,12},{10,... | collective-permute-start | bytes 393224 | tf_op jit(solution)/shard_map/ppermute | solution.py:29

commit v3 on v2

--- a/solution.py
+++ b/solution.py
@@ -232,6 +232,24 @@
     )(*operands)
 
 
+def early_sum(blocks):
+    def body(*refs):
+        total = refs[0][...].astype(jnp.float32)
+        for ref in refs[1:-1]:
+            total = total + ref[...].astype(jnp.float32)
+        refs[-1][...] = total
+
+    return pl.pallas_call(
+        body,
+        out_shape=jax.ShapeDtypeStruct(blocks[0].shape, jnp.float32),
+        in_specs=[VMEM] * len(blocks),
+        out_specs=VMEM,
+        compiler_params=pltpu.CompilerParams(vmem_limit_bytes=LIMIT),
+        cost_estimate=cost(1 << 20, 1 << 20),
+        name="early_sum",
+    )(*blocks)
+
+
 def finish(spread, blocks):
     def body(w_ref, *refs):
         total = refs[0][...].astype(jnp.float32)
@@ -282,10 +300,11 @@
     blocks[0, 2], kept = last_chunks(fs, fh, s, [y2s], own, True, (2, 0))
     second = last_chunks(ns, nh, s, [y2, y2s], own, False, (2, 1, 3, 0), kept)
     blocks[1, 2], blocks[1, 1], blocks[1, 3], across, mine = second
-    arrived = [mine, sent(across, lambda x, y, z, core: (x, y ^ 1, z, core))]
+    last = sent(across, lambda x, y, z, core: (x, y ^ 1, z, core))
+    arrived = ([mine], [])
     for (later, k), block in blocks.items():
-        arrived.append(sent(block, lambda x, y, z, core: (x, y ^ int(core == later), z + k, core)))
-    return finish(spread, arrived)
+        arrived[later].append(sent(block, lambda x, y, z, core: (x, y ^ int(core == later), z + k, core)))
+    return finish(spread, [early_sum(arrived[0]), *arrived[1], last])
 
 
 def solution(mesh):

time: 72.6 us -> 71.5 us (0.985)
  the two profiles are of different devices: /device:TPU:0 before, /device:TPU:1 now
where the time goes in v3:
time: 71.5 us; the launch traced here: 71.3 us
  starting transfers between devices  30.7 us (43%)
  Pallas kernels  25.7 us (36%)
  waiting for transfers between devices  13.2 us (18%)
  local copies, waits for them, and re-layouts  1.59 us (2%)
    ppermute x18, starting transfers between devices, sent(): lax.ppermute(value, AXES, [(i, index(*to(*place(i)))) for i in range(128)])  30.7 us
    pallas_call x7, Pallas kernels, add_chunks(): pl.pallas_call(body, out_shape=[jax.ShapeDtypeStruct((half, members), kin...  18.5 us
    ppermute x18, waiting for transfers between devices, sent(): lax.ppermute(value, AXES, [(i, index(*to(*place(i)))) for i in range(128)])  13.2 us
    pallas_call x3, Pallas kernels, last_chunks(): pl.pallas_call(body, out_shape=[jax.ShapeDtypeStruct((own, members), kind...  2.55 us
    pallas_call x1, Pallas kernels, prepare_state(): pl.pallas_call(body, out_shape=(jax.ShapeDtypeStruct((rows, members), jnp...  2.01 us
    pallas_call x1, Pallas kernels, pack_data(): pl.pallas_call(body, out_shape=jax.ShapeDtypeStruct((rows, 2 * members),...  1.76 us
    unnamed x2, local copies, waits for them, and re-layouts  1.59 us
  transfers between devices with their start and end apart: 18, of which 4 were waited for; matrix products, arithmetic and copies ran while one was open for 0% of the time, Pallas kernels for 32%

profile of v3, /device:TPU:1, one launch (start us, length us, event | category | flops | bytes accessed | tf_op | source)
XLA Modules:
  0.0 71.3 jit_solution(13032493800450761486)
XLA Ops:
  0.0 1.8 %pack_data.1.refs_2_ = bf16[512,512]{1,0:T(8,128)(2,1)S(1)} custom-call(f32[512,256]{1,0:T(8,128)} %p_hbm.1, bf16[512,256]{1,0:T(8,128)(2,1)} %i_hbm.1), custom_call_target="tpu_custom_call" | custom-call | flops 1048576 | bytes 1048576 | tf_op jit(solution)/shard_map/pack_data/pallas_call | solution.py:79
  1.8 3.4 %collective-permute-start.1 = (bf16[512,512]{1,0:T(8,128)(2,1)S(1)}, bf16[512,512]{1,0:T(8,128)(2,1)S(1)}, u32[]{:S(2)}, u32[]{:S(2)}) collective-permute-start(bf16[512,512]{1,0:T(8,128)(2,1)S(1)} %pack_data.1.refs_2_), channel_id=1, source_target_pairs={{0,16},{1,17},{2,18},{3,19},{4,20},{5,21},{6,22},{7,23},{8,56},{9,... | collective-permute-start | bytes 1572872 | tf_op jit(solution)/shard_map/ppermute | solution.py:29
  5.1 1.6 %copy-done = f32[2048,256]{1,0:T(8,128)S(1)} copy-done((f32[2048,256]{1,0:T(8,128)S(1)}, f32[2048,256]{1,0:T(8,128)}, u32[]{:S(2)}) %copy-start) | copy-done | bytes 2097176
  6.7 2.0 %prepare_state.1 = (bf16[2048,256]{1,0:T(8,128)(2,1)S(1)}, f32[256,256]{1,0:T(8,128)S(1)}) custom-call(f32[2048,256]{1,0:T(8,128)S(1)} %copy-done), custom_call_target="tpu_custom_call" | custom-call | flops 16777216 | bytes 4194304 | tf_op jit(solution)/shard_map/prepare_state/pallas_call | solution.py:119
  8.8 2.8 %collective-permute-start.2 = (bf16[512,512]{1,0:T(8,128)(2,1)S(1)}, bf16[512,512]{1,0:T(8,128)(2,1)S(1)}, u32[]{:S(2)}, u32[]{:S(2)}) collective-permute-start(bf16[512,512]{1,0:T(8,128)(2,1)S(1)} %pack_data.1.refs_2_), channel_id=1, source_target_pairs={{0,68},{1,69},{2,70},{3,71},{4,64},{5,65},{6,66},{7,67},{8,76},{9,... | collective-permute-start | bytes 1572872 | tf_op jit(solution)/shard_map/ppermute | solution.py:29
  11.7 3.0 %collective-permute-start.4 = (bf16[512,512]{1,0:T(8,128)(2,1)S(1)}, bf16[512,512]{1,0:T(8,128)(2,1)S(1)}, u32[]{:S(2)}, u32[]{:S(2)}) collective-permute-start(bf16[512,512]{1,0:T(8,128)(2,1)S(1)} %collective-permute-done.1.refs_3_), channel_id=1, source_target_pairs={{0,16},{1,17},{2,18},{3,19},{4,20},{5,21},{6,22},{7,23},{8,56},{9,... | collective-permute-start | bytes 1572872 | tf_op jit(solution)/shard_map/ppermute | solution.py:29
  14.7 8.6 %collective-permute-done.2.refs_6_ = bf16[512,512]{1,0:T(8,128)(2,1)S(1)} collective-permute-done((bf16[512,512]{1,0:T(8,128)(2,1)S(1)}, bf16[512,512]{1,0:T(8,128)(2,1)S(1)}, u32[]{:S(2)}, u32[]{:S(2)}) %collective-permute-start.2) | collective-permute-done | bytes 524320 | tf_op jit(solution)/shard_map/ppermute | solution.py:29
  23.3 1.5 %collective-permute-start.5 = (bf16[512,512]{1,0:T(8,128)(2,1)S(1)}, bf16[512,512]{1,0:T(8,128)(2,1)S(1)}, u32[]{:S(2)}, u32[]{:S(2)}) collective-permute-start(bf16[512,512]{1,0:T(8,128)(2,1)S(1)} %collective-permute-done.2.refs_6_), channel_id=1, source_target_pairs={{0,16},{1,17},{2,18},{3,19},{4,20},{5,21},{6,22},{7,23},{8,56},{9,... | collective-permute-start | bytes 1572872 | tf_op jit(solution)/shard_map/ppermute | solution.py:29
  24.8 2.6 %collective-permute-start.8 = (bf16[512,512]{1,0:T(8,128)(2,1)S(1)}, bf16[512,512]{1,0:T(8,128)(2,1)S(1)}, u32[]{:S(2)}, u32[]{:S(2)}) collective-permute-start(bf16[512,512]{1,0:T(8,128)(2,1)S(1)} %collective-permute-done.4.refs_7_), channel_id=1, source_target_pairs={{0,68},{1,69},{2,70},{3,71},{4,64},{5,65},{6,66},{7,67},{8,76},{9,... | collective-permute-start | bytes 1572872 | tf_op jit(solution)/shard_map/ppermute | solution.py:29
  27.4 4.6 %shard_map.37 = (f32[1024,256]{1,0:T(8,128)S(1)}, f32[1024,256]{1,0:T(8,128)S(1)}, f32[1024,256]{1,0:T(8,128)S(1)}, f32[1024,256]{1,0:T(8,128)S(1)}) custom-call(bf16[2048,256]{1,0:T(8,128)(2,1)S(1)} %get-tuple-element.37.refs_0_.refs_1_.s_ref, bf16[2048,256]{1,0:T(8,128)(2,1)S(1)} %collective-permute-done.refs_1_.refs_3_, ...), custom_call_target="tpu_custom_call" | custom-call | flops 4294967296 | bytes 4194304 | tf_op jit(solution)/shard_map/pallas_call | solution.py:190
  32.0 2.6 %shard_map.38 = (f32[1024,256]{1,0:T(8,128)S(1)}, f32[1024,256]{1,0:T(8,128)S(1)}, f32[1024,256]{1,0:T(8,128)S(1)}, f32[1024,256]{1,0:T(8,128)S(1)}) custom-call(f32[1024,256]{1,0:T(8,128)S(1)} %get-tuple-element.38.refs_0_, ...), custom_call_target="tpu_custom_call", output_to_operand_aliasing={{0}: (0, {}), {1}: (2, {}), {2}: (4, {}), {3}: (5, {})} | custom-call | flops 2147483648 | bytes 4194304 | tf_op jit(solution)/shard_map/pallas_call | solution.py:190
  34.6 5.0 %shard_map.39 = (f32[1024,256]{1,0:T(8,128)S(1)}, f32[1024,256]{1,0:T(8,128)S(1)}, f32[1024,256]{1,0:T(8,128)S(1)}, f32[1024,256]{1,0:T(8,128)S(1)}) custom-call(f32[1024,256]{1,0:T(8,128)S(1)} %get-tuple-element.42.refs_0_, ...), custom_call_target="tpu_custom_call", output_to_operand_aliasing={{0}: (0, {}), {1}: (2, {}), {2}: (4, {}), {3}: (5, {})} | custom-call | flops 4294967296 | bytes 4194304 | tf_op jit(solution)/shard_map/pallas_call | solution.py:190
  39.6 2.8 %shard_map.40 = (f32[1024,256]{1,0:T(8,128)S(1)}, f32[1024,256]{1,0:T(8,128)S(1)}, f32[1024,256]{1,0:T(8,128)S(1)}, f32[1024,256]{1,0:T(8,128)S(1)}) custom-call(f32[1024,256]{1,0:T(8,128)S(1)} %get-tuple-element.46.refs_0_, ...), custom_call_target="tpu_custom_call", output_to_operand_aliasing={{0}: (0, {}), {1}: (2, {}), {2}: (4, {}), {3}: (5, {})} | custom-call | flops 2147483648 | bytes 4194304 | tf_op jit(solution)/shard_map/pallas_call | solution.py:190
  42.4 1.3 %shard_map.42 = (f32[1024,256]{1,0:T(8,128)S(1)}, bf16[1024,256]{1,0:T(8,128)(2,1)S(1)}) custom-call(f32[1024,256]{1,0:T(8,128)S(1)} %get-tuple-element.54.refs_0_, bf16[2048,256]{1,0:T(8,128)(2,1)S(1)} %get-tuple-element.37.refs_0_.refs_1_.s_ref, f32[1024,256]{1,0:T(8,128)S(1)} %get-tuple-element.55.refs_2_, ...), custom_call_target="tpu_custom_call", output_to_operand_aliasing={{0}: (0, {})} | custom-call | flops 1073741824 | bytes 4194304 | tf_op jit(solution)/shard_map/pallas_call | solution.py:190
  43.8 4.9 %collective-permute-start.10 = (bf16[1024,256]{1,0:T(8,128)(2,1)S(1)}, bf16[1024,256]{1,0:T(8,128)(2,1)S(1)}, u32[]{:S(2)}, u32[]{:S(2)}) collective-permute-start(bf16[1024,256]{1,0:T(8,128)(2,1)S(1)} %get-tuple-element.57), channel_id=1, source_target_pairs={{0,8},{1,9},{2,10},{3,11},{4,12},{5,13},{6,14},{7,15},{8,0},{9,1},... | collective-permute-start | bytes 1572872 | tf_op jit(solution)/shard_map/ppermute | solution.py:29
  48.8 1.3 %shard_map.41 = (f32[1024,256]{1,0:T(8,128)S(1)}, bf16[1024,256]{1,0:T(8,128)(2,1)S(1)}) custom-call(f32[1024,256]{1,0:T(8,128)S(1)} %get-tuple-element.50.refs_0_, bf16[2048,256]{1,0:T(8,128)(2,1)S(1)} %get-tuple-element.37.refs_0_.refs_1_.s_ref, f32[1024,256]{1,0:T(8,128)S(1)} %get-tuple-element.51.refs_2_, ...), custom_call_target="tpu_custom_call", output_to_operand_aliasing={{0}: (0, {})} | custom-call | flops 1073741824 | bytes 4194304 | tf_op jit(solution)/shard_map/pallas_call | solution.py:190
  52.1 1.7 %collective-permute-start.11 = (bf16[256,256]{1,0:T(8,128)(2,1)S(1)}, bf16[256,256]{1,0:T(8,128)(2,1)S(1)}, u32[]{:S(2)}, u32[]{:S(2)}) collective-permute-start(bf16[256,256]{1,0:T(8,128)(2,1)S(1)} %get-tuple-element.60), channel_id=1, source_target_pairs={{0,5},{1,6},{2,7},{3,4},{4,1},{5,2},{6,3},{7,0},{8,9},{9,10},{10,1... | collective-permute-start | bytes 393224 | tf_op jit(solution)/shard_map/ppermute | solution.py:29
  53.8 2.2 %collective-permute-start.12 = (bf16[256,256]{1,0:T(8,128)(2,1)S(1)}, bf16[256,256]{1,0:T(8,128)(2,1)S(1)}, u32[]{:S(2)}, u32[]{:S(2)}) collective-permute-start(bf16[256,256]{1,0:T(8,128)(2,1)S(1)} %get-tuple-element.61), channel_id=1, source_target_pairs={{0,7},{1,4},{2,5},{3,6},{4,3},{5,0},{6,1},{7,2},{8,11},{9,8},{10,9... | collective-permute-start | bytes 393224 | tf_op jit(solution)/shard_map/ppermute | solution.py:29
  56.6 1.3 %collective-permute-start.13 = (bf16[256,256]{1,0:T(8,128)(2,1)S(1)}, bf16[256,256]{1,0:T(8,128)(2,1)S(1)}, u32[]{:S(2)}, u32[]{:S(2)}) collective-permute-start(bf16[256,256]{1,0:T(8,128)(2,1)S(1)} %get-tuple-element.62), channel_id=1, source_target_pairs={{0,6},{1,7},{2,4},{3,5},{4,2},{5,3},{6,0},{7,1},{8,10},{9,11},{10,... | collective-permute-start | bytes 393224 | tf_op jit(solution)/shard_map/ppermute | solution.py:29
  57.9 1.4 %shard_map.45 = (bf16[256,256]{1,0:T(8,128)(2,1)S(1)}, bf16[256,256]{1,0:T(8,128)(2,1)S(1)}, bf16[256,256]{1,0:T(8,128)(2,1)S(1)}, bf16[256,256]{1,0:T(8,128)(2,1)S(1)}, f32[256,256]{1,0:T(8,128)S(1)}) custom-call(f32[1024,256]{1,0:T(8,128)S(1)} %get-tuple-element.52.start_ref, bf16[1024,256]{1,0:T(8,128)(2,1)S(1)} %collective-permute-done.7.handed_ref, ...), custom_call_target="tpu_custom_call" | custom-call | flops 1074790400 | bytes 4194304 | tf_op jit(solution)/shard_map/pallas_call | solution.py:225
  59.3 1.7 %collective-permute-start.14 = (bf16[256,256]{1,0:T(8,128)(2,1)S(1)}, bf16[256,256]{1,0:T(8,128)(2,1)S(1)}, u32[]{:S(2)}, u32[]{:S(2)}) collective-permute-start(bf16[256,256]{1,0:T(8,128)(2,1)S(1)} %get-tuple-element.63), channel_id=1, source_target_pairs={{0,2},{1,3},{2,0},{3,1},{4,6},{5,7},{6,4},{7,5},{8,14},{9,15},{10,... | collective-permute-start | bytes 393224 | tf_op jit(solution)/shard_map/ppermute | solution.py:29
  61.5 3.1 %collective-permute-start.16 = (bf16[256,256]{1,0:T(8,128)(2,1)S(1)}, bf16[256,256]{1,0:T(8,128)(2,1)S(1)}, u32[]{:S(2)}, u32[]{:S(2)}) collective-permute-start(bf16[256,256]{1,0:T(8,128)(2,1)S(1)} %get-tuple-element.65), channel_id=1, source_target_pairs={{0,3},{1,0},{2,1},{3,2},{4,7},{5,4},{6,5},{7,6},{8,15},{9,12},{10,... | collective-permute-start | bytes 393224 | tf_op jit(solution)/shard_map/ppermute | solution.py:29
  66.0 1.5 %collective-permute-done.15.refs_2_ = bf16[256,256]{1,0:T(8,128)(2,1)S(1)} collective-permute-done((bf16[256,256]{1,0:T(8,128)(2,1)S(1)}, bf16[256,256]{1,0:T(8,128)(2,1)S(1)}, u32[]{:S(2)}, u32[]{:S(2)}) %collective-permute-start.15) | collective-permute-done | bytes 131104 | tf_op jit(solution)/shard_map/ppermute | solution.py:29
  67.5 2.6 %collective-permute-done.16.refs_3_ = bf16[256,256]{1,0:T(8,128)(2,1)S(1)} collective-permute-done((bf16[256,256]{1,0:T(8,128)(2,1)S(1)}, bf16[256,256]{1,0:T(8,128)(2,1)S(1)}, u32[]{:S(2)}, u32[]{:S(2)}) %collective-permute-start.16) | collective-permute-done | bytes 131104 | tf_op jit(solution)/shard_map/ppermute | solution.py:29
  (28 shorter events, 5.8 us)
Async XLA Ops:
  1.8 9.9 %collective-permute-start.1 = (bf16[512,512]{1,0:T(8,128)(2,1)S(1)}, bf16[512,512]{1,0:T(8,128)(2,1)S(1)}, u32[]{:S(2)}, u32[]{:S(2)}) collective-permute-start(bf16[512,512]{1,0:T(8,128)(2,1)S(1)} %pack_data.1.refs_2_), channel_id=1, source_target_pairs={{0,16},{1,17},{2,18},{3,19},{4,20},{5,21},{6,22},{7,23},{8,56},{9,... | collective-permute-start | bytes 1572872 | tf_op jit(solution)/shard_map/ppermute | solution.py:29
  5.1 1.6 %copy-start = (f32[2048,256]{1,0:T(8,128)S(1)}, f32[2048,256]{1,0:T(8,128)}, u32[]{:S(2)}) copy-start(f32[2048,256]{1,0:T(8,128)} %s_hbm.1) | copy-start | bytes 6291460
  8.7 18.7 %collective-permute-start = (bf16[2048,256]{1,0:T(8,128)(2,1)S(1)}, bf16[2048,256]{1,0:T(8,128)(2,1)S(1)}, u32[]{:S(2)}, u32[]{:S(2)}) collective-permute-start(bf16[2048,256]{1,0:T(8,128)(2,1)S(1)} %get-tuple-element.37.refs_0_.refs_1_.s_ref), channel_id=1, source_target_pairs={{0,8},{1,9},{2,10},{3,11},{4,12},{5,13},{6,14},{7,15},{8,0},{9,1},... | collective-permute-start | bytes 3145736 | tf_op jit(solution)/shard_map/ppermute | solution.py:29
  8.8 14.5 %collective-permute-start.2 = (bf16[512,512]{1,0:T(8,128)(2,1)S(1)}, bf16[512,512]{1,0:T(8,128)(2,1)S(1)}, u32[]{:S(2)}, u32[]{:S(2)}) collective-permute-start(bf16[512,512]{1,0:T(8,128)(2,1)S(1)} %pack_data.1.refs_2_), channel_id=1, source_target_pairs={{0,68},{1,69},{2,70},{3,71},{4,64},{5,65},{6,66},{7,67},{8,76},{9,... | collective-permute-start | bytes 1572872 | tf_op jit(solution)/shard_map/ppermute | solution.py:29
  11.7 13.2 %collective-permute-start.4 = (bf16[512,512]{1,0:T(8,128)(2,1)S(1)}, bf16[512,512]{1,0:T(8,128)(2,1)S(1)}, u32[]{:S(2)}, u32[]{:S(2)}) collective-permute-start(bf16[512,512]{1,0:T(8,128)(2,1)S(1)} %collective-permute-done.1.refs_3_), channel_id=1, source_target_pairs={{0,16},{1,17},{2,18},{3,19},{4,20},{5,21},{6,22},{7,23},{8,56},{9,... | collective-permute-start | bytes 1572872 | tf_op jit(solution)/shard_map/ppermute | solution.py:29
  14.7 19.9 %collective-permute-start.3 = (bf16[512,512]{1,0:T(8,128)(2,1)S(1)}, bf16[512,512]{1,0:T(8,128)(2,1)S(1)}, u32[]{:S(2)}, u32[]{:S(2)}) collective-permute-start(bf16[512,512]{1,0:T(8,128)(2,1)S(1)} %pack_data.1.refs_2_), channel_id=1, source_target_pairs={{0,48},{1,49},{2,50},{3,51},{4,52},{5,53},{6,54},{7,55},{8,24},{9,... | collective-permute-start | bytes 1572872 | tf_op jit(solution)/shard_map/ppermute | solution.py:29
  23.3 16.3 %collective-permute-start.5 = (bf16[512,512]{1,0:T(8,128)(2,1)S(1)}, bf16[512,512]{1,0:T(8,128)(2,1)S(1)}, u32[]{:S(2)}, u32[]{:S(2)}) collective-permute-start(bf16[512,512]{1,0:T(8,128)(2,1)S(1)} %collective-permute-done.2.refs_6_), channel_id=1, source_target_pairs={{0,16},{1,17},{2,18},{3,19},{4,20},{5,21},{6,22},{7,23},{8,56},{9,... | collective-permute-start | bytes 1572872 | tf_op jit(solution)/shard_map/ppermute | solution.py:29
  24.8 17.6 %collective-permute-start.6 = (bf16[512,512]{1,0:T(8,128)(2,1)S(1)}, bf16[512,512]{1,0:T(8,128)(2,1)S(1)}, u32[]{:S(2)}, u32[]{:S(2)}) collective-permute-start(bf16[512,512]{1,0:T(8,128)(2,1)S(1)} %collective-permute-done.2.refs_6_), channel_id=1, source_target_pairs={{0,48},{1,49},{2,50},{3,51},{4,52},{5,53},{6,54},{7,55},{8,24},{9,... | collective-permute-start | bytes 1572872 | tf_op jit(solution)/shard_map/ppermute | solution.py:29
  24.8 23.9 %collective-permute-start.8 = (bf16[512,512]{1,0:T(8,128)(2,1)S(1)}, bf16[512,512]{1,0:T(8,128)(2,1)S(1)}, u32[]{:S(2)}, u32[]{:S(2)}) collective-permute-start(bf16[512,512]{1,0:T(8,128)(2,1)S(1)} %collective-permute-done.4.refs_7_), channel_id=1, source_target_pairs={{0,68},{1,69},{2,70},{3,71},{4,64},{5,65},{6,66},{7,67},{8,76},{9,... | collective-permute-start | bytes 1572872 | tf_op jit(solution)/shard_map/ppermute | solution.py:29
  43.8 7.7 %collective-permute-start.10 = (bf16[1024,256]{1,0:T(8,128)(2,1)S(1)}, bf16[1024,256]{1,0:T(8,128)(2,1)S(1)}, u32[]{:S(2)}, u32[]{:S(2)}) collective-permute-start(bf16[1024,256]{1,0:T(8,128)(2,1)S(1)} %get-tuple-element.57), channel_id=1, source_target_pairs={{0,8},{1,9},{2,10},{3,11},{4,12},{5,13},{6,14},{7,15},{8,0},{9,1},... | collective-permute-start | bytes 1572872 | tf_op jit(solution)/shard_map/ppermute | solution.py:29
  48.7 2.8 %collective-permute-start.9 = (bf16[512,512]{1,0:T(8,128)(2,1)S(1)}, bf16[512,512]{1,0:T(8,128)(2,1)S(1)}, u32[]{:S(2)}, u32[]{:S(2)}) collective-permute-start(bf16[512,512]{1,0:T(8,128)(2,1)S(1)} %collective-permute-done.8.refs_2_.refs_0_), channel_id=1, source_target_pairs={{0,8},{1,9},{2,10},{3,11},{4,12},{5,13},{6,14},{7,15},{8,0},{9,1},... | collective-permute-start | bytes 1572872 | tf_op jit(solution)/shard_map/ppermute | solution.py:29
  50.1 7.8 %collective-permute-start.7 = (bf16[1024,256]{1,0:T(8,128)(2,1)S(1)}, bf16[1024,256]{1,0:T(8,128)(2,1)S(1)}, u32[]{:S(2)}, u32[]{:S(2)}) collective-permute-start(bf16[1024,256]{1,0:T(8,128)(2,1)S(1)} %get-tuple-element.53), channel_id=1, source_target_pairs={{0,8},{1,9},{2,10},{3,11},{4,12},{5,13},{6,14},{7,15},{8,0},{9,1},... | collective-permute-start | bytes 1572872 | tf_op jit(solution)/shard_map/ppermute | solution.py:29
  52.1 9.4 %collective-permute-start.11 = (bf16[256,256]{1,0:T(8,128)(2,1)S(1)}, bf16[256,256]{1,0:T(8,128)(2,1)S(1)}, u32[]{:S(2)}, u32[]{:S(2)}) collective-permute-start(bf16[256,256]{1,0:T(8,128)(2,1)S(1)} %get-tuple-element.60), channel_id=1, source_target_pairs={{0,5},{1,6},{2,7},{3,4},{4,1},{5,2},{6,3},{7,0},{8,9},{9,10},{10,1... | collective-permute-start | bytes 393224 | tf_op jit(solution)/shard_map/ppermute | solution.py:29
  53.8 10.8 %collective-permute-start.12 = (bf16[256,256]{1,0:T(8,128)(2,1)S(1)}, bf16[256,256]{1,0:T(8,128)(2,1)S(1)}, u32[]{:S(2)}, u32[]{:S(2)}) collective-permute-start(bf16[256,256]{1,0:T(8,128)(2,1)S(1)} %get-tuple-element.61), channel_id=1, source_target_pairs={{0,7},{1,4},{2,5},{3,6},{4,3},{5,0},{6,1},{7,2},{8,11},{9,8},{10,9... | collective-permute-start | bytes 393224 | tf_op jit(solution)/shard_map/ppermute | solution.py:29
  56.6 9.3 %collective-permute-start.13 = (bf16[256,256]{1,0:T(8,128)(2,1)S(1)}, bf16[256,256]{1,0:T(8,128)(2,1)S(1)}, u32[]{:S(2)}, u32[]{:S(2)}) collective-permute-start(bf16[256,256]{1,0:T(8,128)(2,1)S(1)} %get-tuple-element.62), channel_id=1, source_target_pairs={{0,6},{1,7},{2,4},{3,5},{4,2},{5,3},{6,0},{7,1},{8,10},{9,11},{10,... | collective-permute-start | bytes 393224 | tf_op jit(solution)/shard_map/ppermute | solution.py:29
  59.3 6.7 %collective-permute-start.14 = (bf16[256,256]{1,0:T(8,128)(2,1)S(1)}, bf16[256,256]{1,0:T(8,128)(2,1)S(1)}, u32[]{:S(2)}, u32[]{:S(2)}) collective-permute-start(bf16[256,256]{1,0:T(8,128)(2,1)S(1)} %get-tuple-element.63), channel_id=1, source_target_pairs={{0,2},{1,3},{2,0},{3,1},{4,6},{5,7},{6,4},{7,5},{8,14},{9,15},{10,... | collective-permute-start | bytes 393224 | tf_op jit(solution)/shard_map/ppermute | solution.py:29
  61.0 6.5 %collective-permute-start.15 = (bf16[256,256]{1,0:T(8,128)(2,1)S(1)}, bf16[256,256]{1,0:T(8,128)(2,1)S(1)}, u32[]{:S(2)}, u32[]{:S(2)}) collective-permute-start(bf16[256,256]{1,0:T(8,128)(2,1)S(1)} %get-tuple-element.64), channel_id=1, source_target_pairs={{0,1},{1,2},{2,3},{3,0},{4,5},{5,6},{6,7},{7,4},{8,13},{9,14},{10,... | collective-permute-start | bytes 393224 | tf_op jit(solution)/shard_map/ppermute | solution.py:29
  61.5 8.6 %collective-permute-start.16 = (bf16[256,256]{1,0:T(8,128)(2,1)S(1)}, bf16[256,256]{1,0:T(8,128)(2,1)S(1)}, u32[]{:S(2)}, u32[]{:S(2)}) collective-permute-start(bf16[256,256]{1,0:T(8,128)(2,1)S(1)} %get-tuple-element.65), channel_id=1, source_target_pairs={{0,3},{1,0},{2,1},{3,2},{4,7},{5,4},{6,5},{7,6},{8,15},{9,12},{10,... | collective-permute-start | bytes 393224 | tf_op jit(solution)/shard_map/ppermute | solution.py:29
  64.6 5.9 %collective-permute-start.17 = (bf16[256,256]{1,0:T(8,128)(2,1)S(1)}, bf16[256,256]{1,0:T(8,128)(2,1)S(1)}, u32[]{:S(2)}, u32[]{:S(2)}) collective-permute-start(bf16[256,256]{1,0:T(8,128)(2,1)S(1)} %get-tuple-element.66), channel_id=1, source_target_pairs={{0,4},{1,5},{2,6},{3,7},{4,0},{5,1},{6,2},{7,3},{8,12},{9,13},{10,... | collective-permute-start | bytes 393224 | tf_op jit(solution)/shard_map/ppermute | solution.py:29
